TPU v7x, 128 devices: a whole 4x4x4 slice. The times are simulated.
128 devices in a mesh: tp: 2 (over core), dp: 64 (over z, y, x).
Axes of the slice: x: 4, y: 4, z: 4, core: 2. Of those that a mesh axis runs over, the one named last changes fastest.
Arguments:
- hidden: bfloat16 [64, 1024, 512], P('dp')
- labels: int32 [64, 1024], P('dp')
- loss_mask: int32 [64, 1024], P('dp')
- ln_gain: float32 [512], replicated
- ln_bias: float32 [512], replicated
- w_query: bfloat16 [512, 8, 64], P(None, 'tp')
- w_key: bfloat16 [512, 8, 64], P(None, 'tp')
- w_value: bfloat16 [512, 8, 64], P(None, 'tp')
- w_attn_out: bfloat16 [8, 64, 512], P('tp')
- w_fc_in: bfloat16 [512, 2048], P(None, 'tp')
- b_fc_in: float32 [2048], P('tp')
- w_fc_out: bfloat16 [2048, 512], P('tp')
- b_fc_out: float32 [512], replicated
- lnf_gain: float32 [512], replicated
- lnf_bias: float32 [512], replicated
- w_head: bfloat16 [512, 50304], P(None, 'tp')
- b_head: float32 [50304], P('tp')
Outputs:
- output 1: float32 [], replicated
- output 2: bfloat16 [64, 1024, 512], P('dp')
- output 3: float32 [512], replicated
- output 4: float32 [512], replicated
- output 5: float32 [512, 8, 64], P(None, 'tp')
- output 6: float32 [512, 8, 64], P(None, 'tp')
- output 7: float32 [512, 8, 64], P(None, 'tp')
- output 8: float32 [8, 64, 512], P('tp')
- output 9: float32 [512, 2048], P(None, 'tp')
- output 10: float32 [2048], P('tp')
- output 11: float32 [2048, 512], P('tp')
- output 12: float32 [512], replicated
- output 13: float32 [512], replicated
- output 14: float32 [512], replicated
- output 15: float32 [512, 50304], P(None, 'tp')
- output 16: float32 [50304], P('tp')
All inputs are finite; a program needn't handle non-finite values.
Results may differ from a plain program's by a relative error of at most 0.0132186.
Values sent between devices are 32-bit elements.
A program may use at most 1 GiB of HBM per device.

v0:
```python
import functools
import jax
import jax.numpy as jnp
from jax import lax
from jax.sharding import PartitionSpec as P

LN_EPS = 1e-5
ROPE_BASE = 10000.0
DATA_SPECS = (P('dp', None, None), P('dp', None), P('dp', None))
PARAM_SPECS = (P(None), P(None), P(None, 'tp', None), P(None, 'tp', None), P(None, 'tp', None),
               P('tp', None, None), P(None, 'tp'), P('tp'), P('tp', None), P(None), P(None), P(None),
               P(None, 'tp'), P('tp'))


def norm_stats(values):
    row_mean = jnp.mean(values, axis=-1, keepdims=True)
    centered = values - row_mean
    inv_std = lax.rsqrt(jnp.mean(centered * centered, axis=-1, keepdims=True) + LN_EPS)
    return centered * inv_std, inv_std


def norm_backward(grad_out, x_hat, inv_std, gain_vec):
    grad_hat = grad_out * gain_vec
    mean_grad = jnp.mean(grad_hat, axis=-1, keepdims=True)
    mean_proj = jnp.mean(grad_hat * x_hat, axis=-1, keepdims=True)
    grad_in = inv_std * (grad_hat - mean_grad - x_hat * mean_proj)
    return grad_in, jnp.sum(grad_out * x_hat, axis=(0, 1)), jnp.sum(grad_out, axis=(0, 1))


def rope_tables(seq_count, rot_dim):
    half_rot = rot_dim // 2
    inv_freq = ROPE_BASE ** (-2.0 * jnp.arange(half_rot, dtype=jnp.float32) / rot_dim)
    angles = jnp.arange(seq_count, dtype=jnp.float32)[:, None] * inv_freq[None, :]
    return jnp.cos(angles)[:, None, :], jnp.sin(angles)[:, None, :]


def apply_rotary(tensor, cosine, sine_tab):
    rot_dim = 2 * cosine.shape[-1]
    pairs = tensor[..., :rot_dim].reshape(tensor.shape[:-1] + (rot_dim // 2, 2))
    even_part = pairs[..., 0]
    odd_part = pairs[..., 1]
    rotated = jnp.stack([even_part * cosine - odd_part * sine_tab, odd_part * cosine + even_part * sine_tab], axis=-1)
    return jnp.concatenate([rotated.reshape(tensor.shape[:-1] + (rot_dim,)), tensor[..., rot_dim:]], axis=-1)


def solution(mesh):
    def local_step(hidden, labels, loss_mask, ln_gain, ln_bias, w_query, w_key, w_value, w_attn_out,
                   w_fc_in, b_fc_in, w_fc_out, b_fc_out, lnf_gain, lnf_bias, w_head, b_head):
        seq_count = hidden.shape[1]
        head_dim = w_query.shape[2]
        vocab_loc = w_head.shape[1]
        score_scale = head_dim ** -0.5
        cosine, sine_tab = rope_tables(seq_count, head_dim // 4)
        causal = jnp.arange(seq_count)[None, :] <= jnp.arange(seq_count)[:, None]
        resid_in = hidden.astype(jnp.float32)
        ln_hat, ln_inv = norm_stats(resid_in)
        normed = (ln_hat * ln_gain + ln_bias).astype(jnp.bfloat16)
        q_rot = apply_rotary(jnp.einsum('btd,dhe->bthe', normed, w_query, preferred_element_type=jnp.float32),
                             cosine, sine_tab).astype(jnp.bfloat16)
        k_rot = apply_rotary(jnp.einsum('btd,dhe->bthe', normed, w_key, preferred_element_type=jnp.float32),
                             cosine, sine_tab).astype(jnp.bfloat16)
        v_proj = jnp.einsum('btd,dhe->bthe', normed, w_value, preferred_element_type=jnp.float32).astype(jnp.bfloat16)
        scores = jnp.einsum('bqhe,bkhe->bhqk', q_rot, k_rot, preferred_element_type=jnp.float32) * score_scale
        probs = jax.nn.softmax(jnp.where(causal, scores, -1e30), axis=-1)
        probs_bf = probs.astype(jnp.bfloat16)
        context = jnp.einsum('bhqk,bkhe->bqhe', probs_bf, v_proj, preferred_element_type=jnp.float32).astype(jnp.bfloat16)
        pre_act = jnp.einsum('btd,df->btf', normed, w_fc_in, preferred_element_type=jnp.float32) + b_fc_in
        gelu_out, gelu_vjp = jax.vjp(functools.partial(jax.nn.gelu, approximate=True), pre_act)
        gelu_bf = gelu_out.astype(jnp.bfloat16)
        block_part = (jnp.einsum('crif,ife->cre', context, w_attn_out, preferred_element_type=jnp.float32)
                      + jnp.einsum('btf,fd->btd', gelu_bf, w_fc_out, preferred_element_type=jnp.float32))
        resid_out = resid_in + lax.psum(block_part, 'tp') + b_fc_out
        fin_hat, fin_inv = norm_stats(resid_out)
        final_bf = (fin_hat * lnf_gain + lnf_bias).astype(jnp.bfloat16)
        logits = jnp.einsum('btd,dv->btv', final_bf, w_head, preferred_element_type=jnp.float32) + b_head
        glob_max = lax.pmax(jnp.max(logits, axis=-1), 'tp')
        local_label = labels - lax.axis_index('tp') * vocab_loc
        is_target = jnp.arange(vocab_loc) == local_label[..., None]
        exp_sum, target_logit = lax.psum((jnp.sum(jnp.exp(logits - glob_max[..., None]), axis=-1),
                                          jnp.sum(jnp.where(is_target, logits, 0.0), axis=-1)), 'tp')
        log_norm = glob_max + jnp.log(exp_sum)
        mask_f = loss_mask.astype(jnp.float32)
        token_count = lax.psum(jnp.sum(mask_f), 'dp')
        tok_weight = mask_f / token_count
        loss_part = jnp.sum(tok_weight * (log_norm - target_logit))
        grad_logits = (jnp.exp(logits - log_norm[..., None]) - jnp.where(is_target, 1.0, 0.0)) * tok_weight[..., None]
        grad_logits_bf = grad_logits.astype(jnp.bfloat16)
        grad_b_head = jnp.sum(grad_logits, axis=(0, 1))
        grad_w_head = jnp.einsum('btd,btv->dv', final_bf, grad_logits_bf, preferred_element_type=jnp.float32)
        grad_final = lax.psum(jnp.einsum('btv,dv->btd', grad_logits_bf, w_head, preferred_element_type=jnp.float32), 'tp')
        grad_resid, grad_lnf_gain, grad_lnf_bias = norm_backward(grad_final, fin_hat, fin_inv, lnf_gain)
        grad_b_fc_out = jnp.sum(grad_resid, axis=(0, 1))
        grad_block = grad_resid.astype(jnp.bfloat16)
        grad_w_fc_out = jnp.einsum('btf,btd->fd', gelu_bf, grad_block, preferred_element_type=jnp.float32)
        grad_gelu = jnp.einsum('btd,fd->btf', grad_block, w_fc_out, preferred_element_type=jnp.float32)
        grad_pre = gelu_vjp(grad_gelu)[0]
        grad_b_fc_in = jnp.sum(grad_pre, axis=(0, 1))
        grad_pre_bf = grad_pre.astype(jnp.bfloat16)
        grad_w_fc_in = jnp.einsum('btd,btf->df', normed, grad_pre_bf, preferred_element_type=jnp.float32)
        grad_w_attn_out = jnp.einsum('crif,cre->ife', context, grad_block, preferred_element_type=jnp.float32)
        grad_context = jnp.einsum('cre,ife->crif', grad_block, w_attn_out, preferred_element_type=jnp.float32).astype(jnp.bfloat16)
        grad_v = jnp.einsum('bhqk,bqhe->bkhe', probs_bf, grad_context, preferred_element_type=jnp.float32).astype(jnp.bfloat16)
        grad_probs = jnp.einsum('bqhe,bkhe->bhqk', grad_context, v_proj, preferred_element_type=jnp.float32)
        grad_scores = (probs * (grad_probs - jnp.sum(grad_probs * probs, axis=-1, keepdims=True)) * score_scale).astype(jnp.bfloat16)
        grad_q = apply_rotary(jnp.einsum('bhqk,bkhe->bqhe', grad_scores, k_rot, preferred_element_type=jnp.float32),
                              cosine, -sine_tab).astype(jnp.bfloat16)
        grad_k = apply_rotary(jnp.einsum('bhqk,bqhe->bkhe', grad_scores, q_rot, preferred_element_type=jnp.float32),
                              cosine, -sine_tab).astype(jnp.bfloat16)
        grad_w_query = jnp.einsum('btd,bthe->dhe', normed, grad_q, preferred_element_type=jnp.float32)
        grad_w_key = jnp.einsum('btd,bthe->dhe', normed, grad_k, preferred_element_type=jnp.float32)
        grad_w_value = jnp.einsum('btd,bthe->dhe', normed, grad_v, preferred_element_type=jnp.float32)
        grad_normed_part = (jnp.einsum('bthe,dhe->btd', grad_q, w_query, preferred_element_type=jnp.float32)
                            + jnp.einsum('bthe,dhe->btd', grad_k, w_key, preferred_element_type=jnp.float32)
                            + jnp.einsum('bthe,dhe->btd', grad_v, w_value, preferred_element_type=jnp.float32)
                            + jnp.einsum('btf,df->btd', grad_pre_bf, w_fc_in, preferred_element_type=jnp.float32))
        grad_normed = lax.psum(grad_normed_part, 'tp')
        grad_ln_in, grad_ln_gain, grad_ln_bias = norm_backward(grad_normed, ln_hat, ln_inv, ln_gain)
        grad_hidden = (grad_resid + grad_ln_in).astype(jnp.bfloat16)
        summed = lax.psum((loss_part, grad_ln_gain, grad_ln_bias, grad_w_query, grad_w_key, grad_w_value,
                           grad_w_attn_out, grad_w_fc_in, grad_b_fc_in, grad_w_fc_out, grad_b_fc_out,
                           grad_lnf_gain, grad_lnf_bias, grad_w_head, grad_b_head), 'dp')
        return (summed[0], grad_hidden) + tuple(summed[1:])

    return jax.shard_map(local_step, mesh=mesh, in_specs=DATA_SPECS + PARAM_SPECS,
                         out_specs=(P(), P('dp', None, None)) + PARAM_SPECS, check_vma=False)
```

profile of v0, /device:TPU:0, one launch (start us, length us, event | category | flops | bytes accessed | tf_op | source)
XLA Modules:
  0.0 1160.5 jit_solution(15712654721603760624)
XLA Ops:
  19.9 3.9 multiply_convert_fusion.1
  23.9 2.6 fusion.113
  26.4 11.1 fusion.108
  37.6 7.5 fusion.60
  48.5 181.1 %psum.147 = f32[]{:T(128)} all-reduce(f32[]{:T(128)} %convert_reduce_fusion.1), channel_id=1, replica_groups=mesh['tp'=2,'dp'=64] {'dp'}, use_global_device_ids=true, to_apply=%region_1.0 | all-reduce | flops 1 | bytes 8 | tf_op jit(solution)/shard_map/psum | solution.py:83
  230.3 1.9 fusion.106
  234.6 46.6 %add_reduce_fusion = (f32[1024]{0:T(1024)S(1)}, f32[1024,25152]{0,1:T(8,128)}) fusion(f32[25152]{0:T(1024)S(1)} %copy-done.25, bf16[512,25152]{0,1:T(8,128)(2,1)} %param.32, bf16[1024,512]{1,0:T(8,128)(2,1)S(1)} %fusion.104.clone.4), kind=kOutput, calls=%fused_computation.6 | convolution fusion | flops 26425294848 | bytes 129931520 | tf_op jit(solution)/shard_map/btd,dv->btv/dot_general | solution.py:75
  281.2 2.4 pmax.7
  283.6 31.8 %exponential_reduce_fusion = f32[1024]{0:T(1024)S(1)} fusion(f32[1024,25152]{0,1:T(8,128)} %get-tuple-element.66, f32[1024]{0:T(1024)S(1)} %bitcast.175, f32[25152]{0:T(1024)S(1)} %copy-done.25), kind=kLoop, calls=%fused_computation.5 | loop fusion | flops 77265920 | bytes 103131392 | tf_op jit(solution)/shard_map/reduce_sum | solution.py:79
  315.5 2.5 psum.149
  318.0 63.3 %fusion.2 = (f32[25152]{0:T(1024)}, f32[1024]{0:T(1024)}, bf16[1024,25152]{0,1:T(8,128)(2,1)}) fusion(f32[1024,25152]{0,1:T(8,128)} %get-tuple-element.66, f32[1024]{0:T(1024)S(1)} %bitcast.177, f32[1024]{0:T(1024)S(1)} %bitcast.174, s32[1024]{0:T(1024)S(1)} %bitcast.178, f32[25152]{0:T(1024)S(1)} %copy-done.25), kind=kLoop, calls=%fused_computation.7 | loop fusion | flops 257530304 | bytes 154751488 | tf_op jit(solution)/shard_map/reduce_sum | solution.py:88
  381.3 37.2 %convolution_bitcast_fusion = f32[1,1024,512]{2,1,0:T(8,128)} fusion(bf16[1024,25152]{0,1:T(8,128)(2,1)} %get-tuple-element.45, bf16[512,25152]{0,1:T(8,128)(2,1)} %param.32), kind=kOutput, calls=%fused_computation.69 | convolution fusion | flops 26373783552 | bytes 79364096 | tf_op jit(solution)/shard_map/btv,dv->btd/dot_general | solution.py:90
  418.6 19.6 %all-reduce.9.cloned.1.call-done = f32[1,1024,512]{2,1,0:T(8,128)} async-done(((f32[1,1024,512]{2,1,0:T(8,128)}), f32[1,1024,512]{2,1,0:T(8,128)}) %all-reduce.9.cloned.1.call-update) | async-done | bytes 2097168 | tf_op jit(solution)/shard_map/psum | solution.py:90
  438.2 3.3 multiply_reduce_fusion.1
  446.1 9.3 fusion.57
  455.4 8.1 fusion.80
  463.5 26.2 %fusion.48 = f32[1,1024,4,64]{1,3,2,0:T(8,128)} fusion(f32[4,1024,1024]{1,2,0:T(8,128)} %fusion.80, bf16[1024,4,48]{0,2,1:T(8,128)(2,1)} %get-tuple-element.72, bf16[1024,4,16]{0,2,1:T(8,128)(2,1)} %concatenate.51, f32[4,1024,1024]{1,2,0:T(8,128)} %get-tuple-element.64, f32[4,1024]{1,0:T(4,128)} %copy-done.60), kind=kOutput, calls=%fused_computation.70 | convolution fusion | flops 567284736 | bytes 35143680 | tf_op jit(solution)/shard_map/bhqk,bkhe->bqhe/dot_general | solution.py:105
  489.7 26.7 %fusion.51 = f32[1,1024,4,64]{1,3,2,0:T(8,128)} fusion(f32[4,1024,1024]{1,2,0:T(8,128)} %fusion.80, bf16[1024,4,48]{0,2,1:T(8,128)(2,1)S(1)} %copy-done.27, bf16[1024,4,16]{0,2,1:T(8,128)(2,1)} %concatenate.48, f32[4,1024,1024]{1,2,0:T(8,128)} %get-tuple-element.64, f32[4,1024]{1,0:T(4,128)} %copy-done.60), kind=kOutput, calls=%fused_computation.71 | convolution fusion | flops 567284736 | bytes 35143680 | tf_op jit(solution)/shard_map/bhqk,bqhe->bkhe/dot_general | solution.py:107
  522.9 6.5 fusion.109
  530.7 2.6 fusion.73
  536.9 2.6 subtract_convert_fusion.1
  550.6 43.1 %fusion.101 = f32[512,25152]{0,1:T(8,128)} fusion(bf16[1024,25152]{0,1:T(8,128)(2,1)} %get-tuple-element.45, f32[1,1024,512]{2,1,0:T(8,128)S(1)} %copy-done.4, f32[512]{0:T(512)} %param.31, f32[512]{0:T(512)S(1)} %copy-done.47, f32[1024]{0:T(1024)S(1)} %copy-done.41, f32[1024]{0:T(1024)S(1)} %copy-done.37), kind=kOutput, calls=%fused_computation.147 | convolution fusion | flops 26376404992 | bytes 105132032 | tf_op jit(solution)/shard_map/btd,btv->dv/dot_general | solution.py:89
  595.9 2.8 fusion.65
  602.4 2.6 fusion.69
  605.0 2.6 fusion.71
  608.2 2.4 psum.150
  611.9 2.7 fusion.40
  614.7 352.9 %all-reduce = (f32[]{:T(128)}, f32[512]{0:T(512)}, f32[512]{0:T(512)}, f32[1024]{0:T(1024)}, f32[512]{0:T(512)}, /*index=5*/f32[512]{0:T(512)}, f32[512]{0:T(512)}) all-reduce(f32[]{:T(128)} %multiply_reduce_fusion.6, f32[512]{0:T(512)S(1)} %get-tuple-element.20, ...), channel_id=1, replica_groups=mesh['tp'=2,'dp'=64] {'dp'}, use_global_device_ids=true, to_apply=%region_16.17 | all-reduce | flops 3585 | bytes 28680 | tf_op jit(solution)/shard_map/psum | solution.py:119
  967.6 3.4 fusion.39
  971.0 136.6 %all-reduce.13.cloned.1.call-done = (f32[512,4,64]{0,2,1:T(8,128)}, f32[512,4,64]{0,2,1:T(8,128)}, f32[512,4,64]{0,2,1:T(8,128)}, f32[4,64,512]{2,1,0:T(8,128)},...) async-done(((f32[512,4,64]{0,2,1:T(8,128)}, f32[512,4,64]{0,2,1:T(8,128)}, f32[512,4,64]{0,2,1:T(8,128)}, ...) | async-done | bytes 57903376 | tf_op jit(solution)/shard_map/psum | solution.py:119
  1107.6 2.0 copy.52
  1117.9 35.1 %copy.58 = f32[512,25152]{0,1:T(8,128)} copy(f32[512,25152]{0,1:T(8,128)} %get-tuple-element.89) | data formatting | bytes 103022592
  (195 shorter events, 62.5 us)
Async XLA Ops:
  7.2 12.7 %copy-start = (bf16[512,1024]{1,0:T(8,128)(2,1)S(1)}, bf16[512,1024]{1,0:T(8,128)(2,1)}, u32[]{:S(2)}) copy-start(bf16[512,1024]{1,0:T(8,128)(2,1)} %param.26) | copy-start | bytes 3145732
  7.2 223.1 %all-reduce.7.cloned.1.call-start = ((), (), s32[]{:S(2)}) async-start(), calls=%async_computation | async-start | bytes 4194304 | tf_op jit(solution)/shard_map/psum | solution.py:72
  12.3 7.6 copy-start.1
  12.8 6.6 copy-start.22
  13.3 6.6 copy-start.57
  16.4 7.5 copy-start.28
  19.9 17.7 %copy-start.9 = (f32[1024,256]{0,1}, f32[1024,256]{0,1:S(1)}, u32[]{:S(2)}) copy-start(f32[1024,256]{0,1:S(1)} %fusion.110) | copy-start | bytes 3145732
  37.6 7.5 copy-start.60
  37.6 8.3 copy-start.17
  37.6 8.3 copy-start.29
  45.9 184.3 %copy-start.53 = (s32[1,1024]{1,0:T(1,128)S(1)}, s32[1,1024]{1,0:T(1,128)}, u32[]{:S(2)}) copy-start(s32[1,1024]{1,0:T(1,128)} %param.18) | copy-start | bytes 12292
  45.9 184.4 %copy-start.5 = (bf16[1,1024,512]{2,1,0:T(8,128)(2,1)S(1)}, bf16[1,1024,512]{2,1,0:T(8,128)(2,1)}, u32[]{:S(2)}) copy-start(bf16[1,1024,512]{2,1,0:T(8,128)(2,1)} %param.17) | copy-start | bytes 3145732
  45.9 184.4 %copy-start.54 = (f32[512]{0:T(512)S(1)}, f32[512]{0:T(512)}, u32[]{:S(2)}) copy-start(f32[512]{0:T(512)} %param.29) | copy-start | bytes 6148
  47.8 186.4 %copy-start.46 = (f32[512]{0:T(512)S(1)}, f32[512]{0:T(512)}, u32[]{:S(2)}) copy-start(f32[512]{0:T(512)} %param.30) | copy-start | bytes 6148
  47.8 186.4 %copy-start.55 = (f32[512]{0:T(512)S(1)}, f32[512]{0:T(512)}, u32[]{:S(2)}) copy-start(f32[512]{0:T(512)} %param.31) | copy-start | bytes 6148
  47.8 390.4 %all-reduce.9.cloned.1.call-start = ((), (), s32[]{:S(2)}) async-start(), calls=%async_computation.1 | async-start | bytes 4194304 | tf_op jit(solution)/shard_map/psum | solution.py:90
  318.0 63.3 %copy-start.42 = (f32[1,1024]{1,0:T(1,128)}, f32[1,1024]{1,0:T(1,128)S(1)}, u32[]{:S(2)}) copy-start(f32[1,1024]{1,0:T(1,128)S(1)} %log_add_fusion) | copy-start | bytes 12292
  381.3 56.9 %copy-start.4 = (f32[1,1024,512]{2,1,0:T(8,128)S(1)}, f32[1,1024,512]{2,1,0:T(8,128)}, u32[]{:S(2)}) copy-start(f32[1,1024,512]{2,1,0:T(8,128)} %copy-done.3) | copy-start | bytes 6291460
  381.3 56.9 %copy-start.37 = (f32[1024]{0:T(1024)S(1)}, f32[1024]{0:T(1024)}, u32[]{:S(2)}) copy-start(f32[1024]{0:T(1024)} %copy-done.36) | copy-start | bytes 12292
  381.3 56.9 %copy-start.41 = (f32[1024]{0:T(1024)S(1)}, f32[1024]{0:T(1024)}, u32[]{:S(2)}) copy-start(f32[1024]{0:T(1024)} %copy-done.40) | copy-start | bytes 12292
  381.3 56.9 %copy-start.47 = (f32[512]{0:T(512)S(1)}, f32[512]{0:T(512)}, u32[]{:S(2)}) copy-start(f32[512]{0:T(512)} %param.30) | copy-start | bytes 6148
  418.5 193.4 %all-reduce.11.cloned.1.call-start = ((), (), s32[]{:S(2)}) async-start(), calls=%async_computation.2 | async-start | bytes 4194304 | tf_op jit(solution)/shard_map/psum | solution.py:116
  446.1 9.3 copy-start.10
  463.5 26.2 %copy-start.27 = (bf16[1024,4,48]{0,2,1:T(8,128)(2,1)S(1)}, bf16[1024,4,48]{0,2,1:T(8,128)(2,1)}, u32[]{:S(2)}) copy-start(bf16[1024,4,48]{0,2,1:T(8,128)(2,1)} %get-tuple-element.71) | copy-start | bytes 1179652
  550.6 557.0 %all-reduce.13.cloned.1.call-start = ((), (), s32[]{:S(2)}) async-start(), calls=%async_computation.3 | async-start | bytes 115810304 | tf_op jit(solution)/shard_map/psum | solution.py:119
  595.9 6.5 copy-start.12
  607.6 7.1 copy-start.50
  607.6 7.1 copy-start.51
  607.6 7.1 copy-start.52
  1107.6 7.6 copy-start.14
  1107.6 8.9 copy-start.13
  1117.9 35.1 %copy-start.33 = (f32[25152]{0:T(1024)S(1)}, f32[25152]{0:T(1024)}, u32[]{:S(2)}) copy-start(f32[25152]{0:T(1024)} %get-tuple-element.90) | copy-start | bytes 301828
  (34 other events, 107.0 us)
Sparse Core Ops, SparseCore 0:
  47.9 28.5 all-reduce.6
  418.6 19.4 all-reduce.8
  550.7 27.4 all-reduce.10
  607.8 499.7 all-reduce.12
where the time goes:
time: 1170 us; the launch traced here: 1160 us
  blocking collectives  541 us (46%)
  matrix products  252 us (22%)
  waiting for transfers between devices  156 us (13%)
  other arithmetic  127 us (11%)
  local copies, waits for them, and re-layouts  68.6 us (6%)
  between operations  15 us (1%)
    psum x1, blocking collectives, local_step(): lax.psum((loss_part, grad_ln_gain, grad_ln_bias, grad_w_query, grad_w_key...  353 us
    psum x1, blocking collectives, local_step(): token_count = lax.psum(jnp.sum(mask_f), 'dp')  181 us
    psum x1, waiting for transfers between devices, local_step(): lax.psum((loss_part, grad_ln_gain, grad_ln_bias, grad_w_query, grad_w_key...  137 us
    reduce_sum x1, other arithmetic, local_step(): grad_b_head = jnp.sum(grad_logits, axis=(0, 1))  63.3 us
    unnamed x132, local copies, waits for them, and re-layouts  52.6 us
    dot_general x1, matrix products, local_step(): jnp.einsum('btd,dv->btv', final_bf, w_head, preferred_element_type=jnp.fl...  46.6 us
    dot_general x1, matrix products, local_step(): jnp.einsum('btd,btv->dv', final_bf, grad_logits_bf, preferred_element_typ...  43.1 us
    dot_general x1, matrix products, local_step(): jnp.einsum('btv,dv->btd', grad_logits_bf, w_head, preferred_element_type=...  37.2 us
  transfers between devices with their start and end apart: 4, of which 2 were waited for; matrix products, arithmetic and copies ran while one was open for 6% of the time, Pallas kernels for 0%

commit v1 on v0

v1 whole, which is shorter than its diff:
```python
import functools
import jax
import jax.numpy as jnp
import numpy as np
from jax import lax
from jax.experimental import pallas as pl
from jax.experimental.pallas import tpu as pltpu
from jax.sharding import Mesh, PartitionSpec as P

F32, BF16 = jnp.float32, jnp.bfloat16
NT = (((1,), (1,)), ((), ()))
NN = (((1,), (0,)), ((), ()))
TN = (((0,), (0,)), ((), ()))
NEG = -1e30
LN_EPS = 1e-5
ROPE_BASE = 10000.0
LANES, SUBLANES = 128, 8
MICROSECOND = 1_000_000_000
ZERO, ONE, TWO, RING = 0, 1, 2, 4
DP = ('z', 'y', 'x')
DATA_SPECS = (P(DP, None, None), P(DP, None), P(DP, None))
PARAM_SPECS = (P(None), P(None), P(None, 'tp', None), P(None, 'tp', None), P(None, 'tp', None),
               P('tp', None, None), P(None, 'tp'), P('tp'), P('tp', None), P(None), P(None), P(None),
               P(None, 'tp'), P('tp'))
TURNS = (1, 3)
RIGHT, LEFT, _ = ([(i, (i + turn) % RING) for i in range(RING)] for turn in (*TURNS, TWO))
SWAP = [(0, 1), (1, 0)]
UNIT = 200
PIECE = RING * UNIT
HALF_SLICE = RING * PIECE
SLICE = TWO * HALF_SLICE
ORDERS = (('x', 'y', 'z'), ('y', 'z', 'x'), ('z', 'x', 'y'))
PARTS = ((72, 0, 0, 0, 0), (64, 72, 0, 0, 1), (64, 136, 0, 1, 0), (64, 0, 1, 1, 1), (64, 64, 1, 2, 0), (72, 128, 1, 2, 1))
BLOCK = ((16, 0), (8, 0), (16, 1), (16, 2))
HALVES = (pl.ds(0, 2), pl.ds(2, 2))
MESH_ID = pl.DeviceIdType.MESH
ANY, WHOLE, SCALARS = (pl.BlockSpec(memory_space=space) for space in (pl.ANY, pltpu.VMEM, pltpu.SMEM))


def dot(a, b, dims):
    return lax.dot_general(a, b, dims, preferred_element_type=F32)


def iota(shape, axis, dtype=jnp.int32):
    return lax.broadcasted_iota(dtype, shape, axis)


def params(collective=None):
    return pltpu.CompilerParams(vmem_limit_bytes=60 * 2 ** 20, collective_id=collective, has_side_effects=collective is not None)


def cost(us, transfer=1):
    return pl.CostEstimate(flops=us * MICROSECOND, bytes_accessed=transfer, transcendentals=1)


def struct(shape, dtype=F32):
    return jax.ShapeDtypeStruct(shape, dtype)


def origin(*_):
    return (0, 0)


def row_block(i, *_):
    return (i, 0)


def column_block(i, *_):
    return (0, i)


def chunks(total, size=LANES):
    return [slice(at, at + size) for at in range(ZERO, total, size)]


def as_row(column):
    return jnp.transpose(jnp.broadcast_to(column, (column.shape[0], LANES)))[0:1]


def head_lse(z, w_t, bias, begin=None, tile=2560, sub=512):
    tokens, dim = z.shape
    vocab = w_t.shape[0]
    steps = pl.cdiv(vocab, tile)
    early = steps // TWO
    offset = ZERO if begin is None else early

    def kernel(z_ref, w_ref, b_ref, *refs):
        step = pl.program_id(ZERO) + offset
        *begins, m_ref, s_ref = refs
        out_ref = begins.pop() if begins else None

        @pl.when(step == offset)
        def _():
            m_ref[...] = begins[0][...] if begins else jnp.full_like(m_ref, NEG)
            s_ref[...] = begins[1][...] if begins else jnp.zeros_like(s_ref)

        def work(last):
            zz = z_ref[...]
            for part in chunks(tile, sub):
                l = dot(zz, w_ref[part, :], NT) + b_ref[:, part]
                if last:
                    l = jnp.where(iota(l.shape, ONE) < vocab - step * tile - part.start, l, NEG)
                lanes = [l[:, c] for c in chunks(sub)]
                m_old = m_ref[...]
                m_new = jnp.maximum(m_old, functools.reduce(jnp.maximum, lanes))
                s_ref[...] = s_ref[...] * jnp.exp(m_old - m_new) + sum(jnp.exp(x - m_new) for x in lanes)
                m_ref[...] = m_new

        pl.when(step < steps - ONE)(lambda: work(last=False))

        @pl.when(step == steps - ONE)
        def _():
            if out_ref is None:
                return
            work(last=True)
            top = jnp.max(m_ref[...], axis=ONE, keepdims=True)
            total = jnp.sum(s_ref[...] * jnp.exp(m_ref[...] - top), axis=ONE, keepdims=True)
            out_ref[0:1] = as_row(top)
            out_ref[1:2] = as_row(total)

    state = pl.BlockSpec((tokens, LANES), origin)
    first = begin is None
    return pl.pallas_call(
        kernel, grid=(early if first else steps - early,),
        in_specs=[pl.BlockSpec((tokens, dim), origin), pl.BlockSpec((tile, dim), lambda i: (i + offset, ZERO)),
                  pl.BlockSpec((ONE, tile), lambda i: (ZERO, i + offset))] + ([] if first else [state] * TWO),
        out_specs=[state] * TWO if first else pl.BlockSpec((TWO, tokens), origin),
        out_shape=[struct((tokens, LANES))] * TWO if first else struct((TWO, tokens)),
        scratch_shapes=[] if first else [pltpu.VMEM((tokens, LANES), F32)] * TWO,
        compiler_params=params(), cost_estimate=cost(19), name='head_lse_first' if first else 'head_lse_rest',
    )(z, w_t, bias, *(begin or ()))


def head_gz(z, w_t, bias, lse, tag, tile=2560, sub=2560):
    tokens, dim = z.shape
    vocab = w_t.shape[0]
    steps = pl.cdiv(vocab, tile)

    def kernel(z_ref, w_ref, b_ref, lse_ref, tag_ref, gz_ref, t_ref, gb_ref):
        step = pl.program_id(ZERO)

        @pl.when(step == ZERO)
        def _():
            gz_ref[...] = jnp.zeros_like(gz_ref)
            t_ref[...] = jnp.zeros_like(t_ref)

        def work(last):
            zz = z_ref[...]
            lane = iota((tokens, LANES), ONE)
            for part in chunks(tile, sub):
                w = w_ref[part, :]
                left = vocab - step * tile - part.start
                if last:
                    w = jnp.where(iota(w.shape, ZERO) < left, w, jnp.zeros_like(w))
                l = dot(zz, w, NT) + b_ref[:, part]
                norm, rel = lse_ref[...], tag_ref[...] - (step * tile + part.start)
                grads, targets = [], []
                for c in chunks(sub):
                    hit = lane == rel - c.start
                    prob = jnp.exp(l[:, c] - norm)
                    if last:
                        prob = jnp.where(lane < left - c.start, prob, 0.0)
                    grads.append(prob - jnp.where(hit, 1.0, 0.0))
                    targets.append(jnp.where(hit, l[:, c], 0.0))
                t_ref[...] += sum(targets)
                grad = jnp.concatenate(grads, axis=ONE)
                gb_ref[:, part] = jnp.sum(grad.reshape(-1, SUBLANES, sub), axis=ZERO)
                gz_ref[...] += dot(grad.astype(BF16), w, NN)

        pl.when(step < steps - ONE)(lambda: work(last=False))
        pl.when(step == steps - ONE)(lambda: work(last=True))

    narrow = pl.BlockSpec((tokens, LANES), origin)
    return pl.pallas_call(
        kernel, grid=(steps,),
        in_specs=[pl.BlockSpec((tokens, dim), origin), pl.BlockSpec((tile, dim), row_block), pl.BlockSpec((ONE, tile), column_block),
                  narrow, narrow],
        out_specs=[pl.BlockSpec((tokens, dim), origin), narrow, pl.BlockSpec((SUBLANES, tile), column_block)],
        out_shape=[struct((tokens, dim)), struct((tokens, LANES)), struct((SUBLANES, steps * tile))],
        compiler_params=params(), cost_estimate=cost(72), name='head_gz',
    )(z, w_t, bias, lse, tag)


def swap_pairs(x, even):
    return jnp.where(even, pltpu.roll(x, LANES - ONE, ONE), pltpu.roll(x, ONE, ONE))


def halves_of(value, low):
    empty = jnp.zeros_like(value)
    return jnp.where(low, value, empty), jnp.where(low, empty, value)


def attn_fwd(u, wq, wk, wv, cos_t, sin_t, scale, blk=256):
    tokens, dim = u.shape
    lanes = wq.shape[0]

    def kernel(u_ref, wq_ref, wk_ref, wv_ref, c_ref, s_ref, qs_ref, k_ref, v_ref, ctx_ref, lse_ref):
        uu, cc, ss = u_ref[...], c_ref[...], s_ref[...]
        even = iota((tokens, LANES), ONE) % TWO == ZERO
        q = dot(uu, wq_ref[...], NT)
        qs_ref[...] = ((q * cc + swap_pairs(q, even) * ss).astype(BF16).astype(F32) * scale).astype(BF16)
        k = dot(uu, wk_ref[...], NT)
        k_ref[...] = (k * cc + swap_pairs(k, even) * ss).astype(BF16)
        v_ref[...] = dot(uu, wv_ref[...], NT).astype(BF16)
        low = iota((blk, LANES), ONE) < LANES // TWO
        causal = iota((blk, blk), ONE) <= iota((blk, blk), ZERO)
        for rows in chunks(tokens, blk):
            before, keys = slice(rows.start), slice(rows.stop)
            out = []
            for h, qh in enumerate(halves_of(qs_ref[rows, :], low)):
                s = jnp.where(causal, dot(qh, k_ref[rows, :], NT), NEG)
                if rows.start:
                    s = jnp.concatenate([dot(qh, k_ref[before, :], NT), s], axis=ONE)
                m = jnp.max(s, axis=ONE, keepdims=True)
                e = jnp.exp(s - m)
                l = jnp.sum(e, axis=ONE, keepdims=True)
                out.append(dot((e * (1.0 / l)).astype(BF16), v_ref[keys, :], NN))
                lse_ref[ZERO, h:h + ONE, rows] = as_row(m + jnp.log(l))
            ctx_ref[rows, :] = jnp.where(low, *out).astype(BF16)

    pair, wide = pl.BlockSpec((tokens, LANES), column_block), pl.BlockSpec((tokens, LANES), origin)
    return pl.pallas_call(
        kernel, grid=(lanes // LANES,),
        in_specs=[pl.BlockSpec((tokens, dim), origin)] + [pl.BlockSpec((LANES, dim), row_block)] * 3 + [wide] * TWO,
        out_specs=[pair] * RING + [pl.BlockSpec((ONE, TWO, tokens), lambda g: (g, ZERO, ZERO))],
        out_shape=[struct((tokens, lanes), BF16)] * RING + [struct((lanes // LANES, TWO, tokens))],
        compiler_params=params(), cost_estimate=cost(13), name='attn_fwd',
    )(u, wq, wk, wv, cos_t, sin_t)


def attn_bwd(qs, k, v, dctx, lse, cos_t, sin_t, scale, blk=256):
    tokens, lanes = qs.shape

    def kernel(qs_ref, k_ref, v_ref, do_ref, lse_ref, c_ref, s_ref, dq_ref, dk_ref, dv_ref, dka_ref, dva_ref):
        low = iota((blk, LANES), ONE) < LANES // TWO
        causal = iota((blk, blk), ZERO) <= iota((blk, blk), ONE)
        even = iota((blk, LANES), ONE) % TWO == ZERO

        def unrotate(x, rows):
            return (x * c_ref[rows, :] - swap_pairs(x, even) * s_ref[rows, :]).astype(BF16)

        dka_ref[...] = jnp.zeros_like(dka_ref)
        dva_ref[...] = jnp.zeros_like(dva_ref)
        for rows in chunks(tokens, blk):
            before, keys = slice(rows.start), slice(rows.stop)
            dqs = []
            for h, (qh, doh) in enumerate(zip(halves_of(qs_ref[rows, :], low), halves_of(do_ref[rows, :], low))):
                norm = lse_ref[ZERO, h:h + ONE, rows]
                p = jnp.where(causal, jnp.exp(dot(k_ref[rows, :], qh, NT) - norm), 0.0)
                if rows.start:
                    p = jnp.concatenate([jnp.exp(dot(k_ref[before, :], qh, NT) - norm), p], axis=ZERO)
                dp = dot(v_ref[keys, :], doh, NT)
                ds = (p * (dp - jnp.sum(p * dp, axis=ZERO, keepdims=True))).astype(BF16)
                dva_ref[keys, :] += dot(p.astype(BF16), doh, NN)
                dka_ref[keys, :] += dot(ds, qh, NN)
                dqs.append(dot(ds, k_ref[keys, :], TN))
            dq_ref[rows, :] = unrotate(jnp.where(low, *dqs) * scale, rows)
        for rows in chunks(tokens, blk):
            dk_ref[rows, :] = unrotate(dka_ref[rows, :], rows)
            dv_ref[rows, :] = dva_ref[rows, :].astype(BF16)

    pair, wide = pl.BlockSpec((tokens, LANES), column_block), pl.BlockSpec((tokens, LANES), origin)
    return pl.pallas_call(
        kernel, grid=(lanes // LANES,),
        in_specs=[pair] * RING + [pl.BlockSpec((ONE, TWO, tokens), lambda g: (g, ZERO, ZERO))] + [wide] * TWO,
        out_specs=[pair] * 3, out_shape=[struct((tokens, lanes), BF16)] * 3,
        scratch_shapes=[pltpu.VMEM((tokens, LANES), F32)] * TWO,
        compiler_params=params(), cost_estimate=cost(13), name='attn_bwd',
    )(qs, k, v, dctx, lse, cos_t, sin_t)


class Wires:
    def __init__(self, send, recv):
        self.send, self.recv, self.all = send, recv, []

    def line(self, src, dst, axis, turn):
        n = len(self.all)

        def build():
            size = TWO if axis == 'tp' else RING
            peer = {axis: lax.rem(lax.axis_index(axis) + turn, size)}
            return pltpu.make_async_remote_copy(src(), dst(), self.send.at[n], self.recv.at[n], device_id=peer, device_id_type=MESH_ID)

        self.all.append(build)
        return build

    def finish(self):
        for build in self.all:
            build().wait_send()


def start(lines):
    for build in lines:
        build().start()


def arrive(lines):
    for build in lines:
        build().wait_recv()


def greet(peers):
    barrier = pltpu.get_barrier_semaphore()
    for peer in peers:
        where = {axis: lax.rem(lax.axis_index(axis) + turn, TWO if axis == 'tp' else RING) for axis, turn in peer}
        pl.semaphore_signal(barrier, device_id=where, device_id_type=MESH_ID)
    return lambda: pl.semaphore_wait(barrier, len(peers))


class RingSum:
    def __init__(self, wires, axis, piece, halves, near, far):
        self.piece, self.halves, self.near, self.far = piece, halves, near, far
        sent = lambda part, s, turn: piece(turn).at[part[s]]
        kept = lambda part, s: far[s].at[part[s]]
        self.first = [wires.line(functools.partial(sent, halves, s, TWO), functools.partial(lambda s: near[s], s), axis, turn)
                      for s, turn in enumerate(TURNS)]
        self.plain, self.added = ([wires.line(functools.partial(sent, part, s, turn), functools.partial(kept, part, s), axis, turn)
                                   for s, turn in enumerate(TURNS)] for part in (halves[::-1], halves))

    def relay(self):
        for s, turn in enumerate(TURNS):
            arrive([self.first[s]])
            part = self.piece(turn).at[self.halves[s]]
            part[...] = part[...] + self.near[s][...]
            start([self.added[s]])

    def result(self):
        arrive(self.plain + self.added)
        return self.piece(ZERO)[...] + (self.far[0][...] + self.far[1][...])


class FanSum:
    def __init__(self, wires, axis, piece, landing):
        self.piece, self.landing = piece, landing
        self.lines = [wires.line(functools.partial(piece, turn), functools.partial(lambda n: landing.at[n], turn - ONE), axis, turn)
                      for turn in range(ONE, RING)]

    def result(self):
        arrive(self.lines)
        return self.piece(ZERO)[...] + (self.landing[0] + self.landing[1] + self.landing[2])


class RingGather:
    def __init__(self, wires, axis, place, relays):
        here = functools.partial(place, ZERO)
        self.step = [wires.line(here, here, axis, turn) for turn in TURNS]
        self.came, self.relays = [], []
        for way, part in relays:
            passed = functools.partial(lambda way, part: place(TURNS[ONE - way]).at[part], way, part)
            self.relays.append((way, wires.line(passed, passed, axis, TURNS[way])))
        self.idle = [s for s in range(TWO) if s not in dict(relays)]

    def forward(self):
        for way, line in self.relays:
            arrive([self.step[way]])
            start([line])

    def result(self):
        arrive([self.step[s] for s in self.idle] + [line for _, line in self.relays])


class FanGather:
    def __init__(self, wires, axis, place):
        here = functools.partial(place, ZERO)
        self.step = [wires.line(here, here, axis, turn) for turn in range(ONE, RING)]

    def result(self):
        arrive(self.step)


def coordinates():
    at = {axis: lax.axis_index(axis) for axis in DP}
    return at, lambda axis, turn: lax.rem(at[axis] + turn, RING)


def head_gw(stats, packets, w_t, bias_cols):
    tokens = stats.shape[1]
    dim = w_t.shape[1]
    vocab = w_t.shape[0]
    half = tokens // TWO
    low = 104
    halves = (pl.ds(ZERO, low), pl.ds(low, UNIT - low))
    colors = (('y', 'z'), ('z', 'y'))
    group = [(x, c) for c in range(TWO) for x in range(RING)][1:]
    firsts = [ZERO] * RING + [packets[3].shape[0]]

    def spot(ref, n):
        return ref.at[min(n, 3), pl.ds(firsts[n], packets[n].shape[0])]

    def kernel(stats_ref, *refs):
        packet_refs, (w_ref, bias_ref), refs = refs[:len(packets)], refs[len(packets):len(packets) + TWO], refs[len(packets) + TWO:]
        outs, (count_out, norm_out), refs = refs[:len(PARTS)], refs[len(PARTS):len(PARTS) + TWO], refs[len(PARTS) + TWO:]
        (acc, w_all, zb, own, theirs, heard, norms, tags, shard, tally, *lanes, send, recv, local) = refs
        at, beside = coordinates()
        tp = lax.axis_index('tp')
        wires = Wires(send, recv)

        entered = greet([(('x', x), ('tp', c)) for x, c in group] + [((a, t),) for a in ('y', 'z') for t in range(ONE, RING)])
        loads = [pltpu.make_async_copy(ref, spot(own, n), local.at[n]) for n, ref in enumerate(packet_refs)]
        for load in loads:
            load.start()
        for n in range(TWO * RING):
            row = pl.multiple_of(at['x'] * SLICE + n * PIECE, 32)
            whole = row + PIECE <= vocab

            @pl.when(whole)
            def _():
                pltpu.make_async_copy(w_ref.at[pl.ds(row, PIECE)], w_all.at[n], local.at[len(packets) + n]).start()

            @pl.when(jnp.logical_not(whole))
            def _():
                pltpu.make_async_copy(w_ref.at[pl.ds(row, vocab % PIECE)], w_all.at[n, pl.ds(ZERO, vocab % PIECE)], local.at[len(packets) + n]).start()
        entered()
        news = []
        for n, (x, c) in enumerate(group):
            where = {'x': beside('x', x), 'tp': lax.rem(tp + c, TWO)}
            news.append(pltpu.make_async_remote_copy(stats_ref, heard.at[n + ONE], send.at[n], recv.at[n], device_id=where, device_id_type=MESH_ID))
            wires.all.append(functools.partial(lambda n: news[n], n))
            news[n].start()
        swaps = [wires.line(functools.partial(lambda n: packet_refs[n], n), functools.partial(spot, theirs, n), 'tp', ONE)
                 for n in range(len(packets))]
        start(swaps)
        mine = pl.multiple_of(tp * half, half)
        other = pl.multiple_of(half - tp * half, half)
        for load in loads:
            load.wait()
        for r in range(RING):
            zb[r, pl.ds(mine, half), :] = own[r, ZERO:half].astype(BF16)
        for copy in news:
            copy.wait_recv()
        heard[0] = stats_ref[...]
        for r, turn in enumerate((0, 1, 3, 2)):
            a, b = heard[turn], heard[turn + RING]
            top = jnp.maximum(a[0:1], b[0:1])
            norm = top + jnp.log(a[1:2] * jnp.exp(a[0:1] - top) + b[1:2] * jnp.exp(b[0:1] - top))
            label, mask = (jnp.concatenate([own[r, half + n:half + n + ONE] for n in (row, row + ONE)], axis=ONE) for row in (ZERO, TWO))
            norms[r] = jnp.where(mask > 0.0, norm, -NEG)
            tags[r] = jnp.where(mask > 0.0, label - (tp * vocab).astype(F32), NEG)
            seen = jnp.broadcast_to(jnp.sum(mask, axis=ONE, keepdims=True), tally.shape[1:])
            tally[6] = seen if r == ZERO else tally[6] + seen
            if r == ZERO:
                norm_out[...] = norm
        arrive(swaps)
        for r in range(RING):
            zb[r, pl.ds(other, half), :] = theirs[r, ZERO:half].astype(BF16)

        pieces = [functools.partial(lambda c, axis, turn: acc.at[c * RING + beside(axis, turn)], c, axis) for c, (axis, _) in enumerate(colors)]
        sums = [RingSum(wires, colors[c][0], pieces[c], HALVES, [lanes[0].at[c], lanes[1].at[c]], [lanes[2].at[c], lanes[3].at[c]])
                for c in range(TWO)]
        votes = FanSum(wires, 'y', lambda turn: tally.at[6], tally.at[pl.ds(0, 3)])

        def unit(u, carry):
            c, turn = lax.rem(u, TWO), lax.div(u, TWO)
            ahead = lax.rem(2 + 3 * turn + 3 * lax.div(turn * (turn - ONE), TWO), RING)
            p = c * RING + lax.rem(at['y'] + (at['z'] - at['y']) * c + ahead, RING)
            first_row = at['x'] * SLICE + p * PIECE
            whole = first_row + PIECE <= vocab

            @pl.when(whole)
            def _():
                pltpu.make_async_copy(w_ref.at[pl.ds(ZERO, PIECE)], w_all.at[p], local.at[len(packets) + p]).wait()

            @pl.when(jnp.logical_not(whole))
            def _():
                pltpu.make_async_copy(w_ref.at[pl.ds(ZERO, vocab % PIECE)], w_all.at[p, pl.ds(ZERO, vocab % PIECE)], local.at[len(packets) + p]).wait()

            w, bias = w_all[p], bias_ref[p]
            row = (iota((PIECE, LANES), ZERO) + first_row).astype(F32)

            logits = dot(w, zb[0], NT)
            for r in range(RING):
                zr, norm, tag, l = zb[r], norms[r], tags[r], logits
                if r + ONE < RING:
                    logits = dot(w, zb[r + ONE], NT)
                grads = []
                for part in chunks(tokens):
                    prob = jnp.exp(l[:, part] + bias - norm[:, part])
                    grads.append((prob - jnp.where(row == tag[:, part], 1.0, 0.0)).astype(BF16))
                out = dot(jnp.concatenate(grads, axis=ONE), zr, NN).reshape(RING, UNIT, dim)
                acc[p] = acc[p] + out if r else out
            for c, total in enumerate(sums):
                pl.when(u == c)(functools.partial(start, total.first))
                pl.when(u == c + TWO)(functools.partial(start, total.plain[:1]))

                @pl.when(u == c + RING)
                def _(total=total):
                    start(total.plain[1:])
                    total.relay()

            return carry

        start(votes.lines)
        lax.fori_loop(ZERO, TWO * RING, unit, ZERO)
        tally[7] = votes.result()
        votes = FanSum(wires, 'z', lambda turn: tally.at[7], tally.at[pl.ds(3, 3)])
        start(votes.lines)

        seconds = []
        for c, (axis, side) in enumerate(colors):
            kept = c * RING + at[axis]
            acc[kept] = sums[c].result()
            seconds.append(RingSum(wires, side, functools.partial(lambda kept, side, turn: acc.at[kept, beside(side, turn)], kept, side),
                                   halves, [lanes[4].at[c], lanes[5].at[c]], [lanes[6].at[c], lanes[7].at[c]]))
            start(seconds[c].first + seconds[c].plain)
        for total in seconds:
            total.relay()
        for c, total in enumerate(seconds):
            shard[c] = total.result()
        count_out[...] = votes.result()

        keep, steps = [], []
        for n, (rows, offset, c, order, way) in enumerate(PARTS):
            a1, a2, _ = ORDERS[order]
            source = shard.at[c, pl.ds(offset, rows)]
            home = functools.partial(lambda n, a1, a2, turn: outs[n].at[at[a2], beside(a1, turn)], n, a1, a2)
            keep.append(pltpu.make_async_copy(source, home(ZERO), local.at[len(packets) + TWO * RING + n]))
            keep[n].start()
            gather = RingGather(wires, a1, home, [(way, pl.ds(ZERO, rows))])
            steps.append(gather)
        for copy in keep:
            copy.wait()
        for gather in steps:
            start(gather.step)
        for gather in steps:
            gather.forward()
        nexts = []
        for n, (rows, _, _, order, way) in enumerate(PARTS):
            _, a2, _ = ORDERS[order]
            steps[n].result()
            nexts.append(RingGather(wires, a2, functools.partial(lambda n, a2, turn: outs[n].at[beside(a2, turn)], n, a2), [(way, pl.ds(ZERO, RING))]))
            start(nexts[n].step)
        for gather in nexts:
            gather.forward()
        for gather in nexts:
            gather.result()
        wires.finish()

    copies = len(group) + len(packets) + TWO * 3 + TWO * TWO * 6 + len(PARTS) * TWO * 3
    row_vector = pltpu.VMEM((RING, ONE, tokens), F32)
    packet = pltpu.VMEM((RING, *packets[0].shape), F32)
    lane = lambda *shape: [pltpu.VMEM((TWO, *shape, dim), F32)]
    return pl.pallas_call(
        kernel, in_specs=[WHOLE] + [ANY] * len(packets) + [ANY, WHOLE], out_specs=[ANY] * len(PARTS) + [WHOLE] * TWO,
        out_shape=[struct((RING, RING, part[0], dim)) for part in PARTS] + [struct((SUBLANES, LANES)), struct((ONE, tokens))],
        scratch_shapes=[pltpu.VMEM((TWO * RING, RING, UNIT, dim), F32), pltpu.VMEM((TWO * RING, PIECE, dim), BF16),
                        pltpu.VMEM((RING, tokens, dim), BF16), packet, packet, pltpu.VMEM((TWO * RING, TWO, tokens), F32),
                        row_vector, row_vector, pltpu.VMEM((TWO, UNIT, dim), F32), pltpu.VMEM((TWO * RING, SUBLANES, LANES), F32),
                        *lane(TWO, UNIT) * TWO, *lane(RING, UNIT) * TWO, *lane(low), *lane(UNIT - low), *lane(UNIT) * TWO,
                        pltpu.SemaphoreType.DMA((copies,)), pltpu.SemaphoreType.DMA((copies,)),
                        pltpu.SemaphoreType.DMA((len(packets) + TWO * RING + len(PARTS),))],
        compiler_params=params(1), cost_estimate=cost(160), name='head_gw',
    )(stats, *packets, w_t, bias_cols)


def chip_sum(inputs):
    count = len(BLOCK)
    flat = [piece for group in inputs for piece in group]
    dim = flat[0].shape[-1]

    def kernel(*refs):
        ins, outs, refs = refs[:len(flat)], refs[len(flat):len(flat) + count], refs[len(flat) + count:]
        acc, bufs, (send, recv, local) = refs[:count], [refs[count * n:count * (n + ONE)] for n in range(ONE, 7)], refs[-3:]
        at, beside = coordinates()
        wires = Wires(send, recv)
        entered = greet([((a, t),) for a in DP for t in range(ONE, RING)])
        loads, used = [[] for _ in BLOCK], ZERO
        for k, group in enumerate(inputs):
            row = ZERO
            for piece in group:
                rows = piece.shape[0]
                loads[k].append(pltpu.make_async_copy(ins[used], acc[k].at[pl.ds(row, rows)], local.at[used]))
                loads[k][-1].start()
                row, used = row + rows, used + ONE
        entered()
        stages = []
        for k, (_, order) in enumerate(BLOCK):
            a1 = ORDERS[order][0]
            stages.append(RingSum(wires, a1, functools.partial(lambda k, a1, turn: acc[k].at[beside(a1, turn)], k, a1),
                                  HALVES, [bufs[0][k], bufs[1][k]], [bufs[2][k], bufs[3][k]]))
            for load in loads[k]:
                load.wait()
            start(stages[k].first + stages[k].plain)
        for stage in stages:
            stage.relay()
        for k, (_, order) in enumerate(BLOCK):
            a1, a2, _ = ORDERS[order]
            acc[k][at[a1]] = stages[k].result()
            stages[k] = FanSum(wires, a2, functools.partial(lambda k, a1, a2, turn: acc[k].at[at[a1], beside(a2, turn)], k, a1, a2), bufs[4][k])
            start(stages[k].lines)
        for k, (_, order) in enumerate(BLOCK):
            a1, a2, a3 = ORDERS[order]
            acc[k][at[a1], at[a2]] = stages[k].result()
            stages[k] = FanSum(wires, a3, functools.partial(lambda k, a1, a2, a3, turn: acc[k].at[at[a1], at[a2], beside(a3, turn)], k, a1, a2, a3), bufs[5][k])
            start(stages[k].lines)
        for k, (_, order) in enumerate(BLOCK):
            a1, a2, a3 = ORDERS[order]
            outs[k][at[a1], at[a2], at[a3]] = stages[k].result()
            stages[k] = FanGather(wires, a3, functools.partial(lambda k, a1, a2, a3, turn: outs[k].at[at[a1], at[a2], beside(a3, turn)], k, a1, a2, a3))
            start(stages[k].step)
        for k, (_, order) in enumerate(BLOCK):
            a1, a2, _ = ORDERS[order]
            stages[k].result()
            stages[k] = FanGather(wires, a2, functools.partial(lambda k, a1, a2, turn: outs[k].at[at[a1], beside(a2, turn)], k, a1, a2))
            start(stages[k].step)
        for k, (_, order) in enumerate(BLOCK):
            a1 = ORDERS[order][0]
            stages[k].result()
            stages[k] = RingGather(wires, a1, functools.partial(lambda k, a1, turn: outs[k].at[beside(a1, turn)], k, a1), list(enumerate(HALVES)))
            start(stages[k].step)
        for stage in stages:
            stage.forward()
        for stage in stages:
            stage.result()
        wires.finish()

    copies = count * (6 + 3 * RING + RING)

    def buffers(*shape):
        return [pltpu.VMEM((*shape, rows, dim), F32) for rows, _ in BLOCK]

    return pl.pallas_call(
        kernel, in_specs=[ANY] * len(flat), out_specs=[WHOLE] * count,
        out_shape=[struct((RING, RING, RING, rows, dim)) for rows, _ in BLOCK],
        scratch_shapes=[*buffers(RING, RING, RING), *buffers(TWO, RING) * TWO, *buffers(RING, RING) * TWO, *buffers(3, RING), *buffers(3),
                        pltpu.SemaphoreType.DMA((copies,)), pltpu.SemaphoreType.DMA((copies,)), pltpu.SemaphoreType.DMA((len(flat),))],
        compiler_params=params(2), cost_estimate=cost(60), name='chip_sum',
    )(*flat)


def place(groups, scale, coords, vocab, into=None):
    jobs = [(shift, n, array) for shift, arrays in groups for n, array in arrays.items()]
    dim = jobs[0][-1].shape[-1]
    steps = RING * RING
    kept = () if into is None else (into,)

    def kernel(coord_ref, scale_ref, *refs):
        ins, (out_ref, bufs, sems) = refs[:len(jobs)], refs[-3:]
        step = pl.program_id(ZERO)

        def each(step, act):
            slot = lax.rem(step, TWO)
            for j, (shift, n, _) in enumerate(jobs):
                rows, offset, c, order, _ = PARTS[n]
                a1, a2, a3 = ORDERS[order]
                at = {a1: lax.rem(step, RING), a2: lax.div(step, RING), a3: lax.rem(coord_ref[DP.index(a3)] + shift, RING)}
                first, second = (('y', 'z'), ('z', 'y'))[c]
                row = pl.multiple_of(at['x'] * SLICE + c * HALF_SLICE + at[first] * PIECE + at[second] * UNIT + offset, SUBLANES)
                edge = vocab % UNIT - offset
                whole = row + rows <= vocab

                def move(size):
                    act(pltpu.make_async_copy(bufs.at[slot, j, pl.ds(ZERO, size)], out_ref.at[pl.ds(row, size)], sems.at[slot, j]))

                pl.when(whole)(functools.partial(move, rows))
                if ZERO < edge < rows:
                    pl.when(jnp.logical_and(row < vocab, jnp.logical_not(whole)))(functools.partial(move, edge))

        @pl.when(step >= TWO)
        def _():
            each(step - TWO, lambda copy: copy.wait())

        for j, (_, n, _) in enumerate(jobs):
            bufs[lax.rem(step, TWO), j, ZERO:PARTS[n][0]] = ins[j][ZERO, ZERO] * scale_ref[ZERO]
        each(step, lambda copy: copy.start())

        @pl.when(step == steps - ONE)
        def _():
            each(step - ONE, lambda copy: copy.wait())
            each(step, lambda copy: copy.wait())

    blocks = [pl.BlockSpec((ONE, ONE, PARTS[n][0], dim), lambda i: (i // RING, i % RING, ZERO, ZERO)) for _, n, _ in jobs]
    return pl.pallas_call(
        kernel, grid=(steps,), in_specs=[SCALARS, SCALARS, *blocks] + [ANY for _ in kept], out_specs=ANY,
        out_shape=struct((vocab, dim)), input_output_aliases={TWO + len(jobs): ZERO for _ in kept},
        scratch_shapes=[pltpu.VMEM((TWO, len(jobs), 72, dim), F32), pltpu.SemaphoreType.DMA((TWO, len(jobs)))],
        compiler_params=params(), cost_estimate=cost(2 * len(jobs)),
    )(coords, scale, *[array for *_, array in jobs], *kept)


def norm_stats(values):
    row_mean = jnp.mean(values, axis=-ONE, keepdims=True)
    centered = values - row_mean
    inv_std = lax.rsqrt(jnp.mean(centered * centered, axis=-ONE, keepdims=True) + LN_EPS)
    return centered * inv_std, inv_std


def norm_backward(grad_out, x_hat, inv_std, gain_vec):
    grad_hat = grad_out * gain_vec
    mean_grad = jnp.mean(grad_hat, axis=-ONE, keepdims=True)
    mean_proj = jnp.mean(grad_hat * x_hat, axis=-ONE, keepdims=True)
    grad_in = inv_std * (grad_hat - mean_grad - x_hat * mean_proj)
    return grad_in, jnp.sum(grad_out * x_hat, axis=ZERO), jnp.sum(grad_out, axis=ZERO)


def rope_tables(tokens, head_dim):
    rot = head_dim // 4
    inv_freq = (ROPE_BASE ** (-2.0 * np.arange(rot // TWO) / rot)).astype(np.float32)
    angles = (np.arange(tokens, dtype=np.float32)[:, np.newaxis] * inv_freq).astype(np.float64)
    cosine, sine = np.ones((tokens, head_dim), np.float32), np.zeros((tokens, head_dim), np.float32)
    cosine[:, :rot] = np.repeat(np.cos(angles), TWO, axis=ONE)
    sine[:, :rot] = np.repeat(np.sin(angles), TWO, axis=ONE) * np.tile([-1.0, 1.0], rot // TWO)
    return [np.tile(table, (ONE, LANES // head_dim)) for table in (cosine, sine)]


def hop(value, axis, way):
    return lax.ppermute(value, axis, way)


def solution(mesh):
    mesh = Mesh(mesh.devices.reshape(TWO, RING, RING, RING), ('tp', *DP))

    def local_step(hidden, labels, loss_mask, ln_gain, ln_bias, w_query, w_key, w_value, w_attn_out,
                   w_fc_in, b_fc_in, w_fc_out, b_fc_out, lnf_gain, lnf_bias, w_head, b_head):
        _, tokens, dim = hidden.shape
        _, heads, head_dim = w_query.shape
        lanes, half = heads * head_dim, tokens // TWO
        vocab = b_head.shape[0]
        score_scale = head_dim ** -0.5
        tp = lax.axis_index('tp')
        swap = lambda value: lax.ppermute(value, 'tp', SWAP)
        rows_of = lambda w: jnp.moveaxis(w, ZERO, -ONE).reshape(lanes, dim)
        wq, wk, wv = rows_of(w_query), rows_of(w_key), rows_of(w_value)
        wo = w_attn_out.reshape(lanes, dim)
        w_t = w_head.T
        tables = rope_tables(tokens, head_dim)
        mask_f = loss_mask.astype(F32)

        resid_in = hidden[ZERO].astype(F32)
        ln_hat, ln_inv = norm_stats(resid_in)
        normed = (ln_hat * ln_gain + ln_bias).astype(BF16)
        qs, k_rot, v_proj, context, lse_att = attn_fwd(normed, wq, wk, wv, *tables, score_scale)
        pre_act = dot(normed, w_fc_in, NN) + b_fc_in
        gelu_out, gelu_vjp = jax.vjp(functools.partial(jax.nn.gelu, approximate=True), pre_act)
        gelu_bf = gelu_out.astype(BF16)
        block_part = dot(context, wo, NN) + dot(gelu_bf, w_fc_out, NN)
        resid_out = resid_in + (block_part + swap(block_part)) + b_fc_out
        fin_hat, fin_inv = norm_stats(resid_out)
        final_f32 = fin_hat * lnf_gain + lnf_bias
        final_bf = final_f32.astype(BF16)

        extra = jnp.concatenate([labels.astype(F32).reshape(TWO, half), mask_f.reshape(TWO, half), jnp.zeros((RING, half), F32)])
        packet = jnp.concatenate([lax.dynamic_slice_in_dim(final_f32, tp * half, half, ZERO), extra])
        from_sides = [hop(packet, 'x', way) for way in (RIGHT, LEFT)]
        cut = packet.shape[0] // TWO // SUBLANES * SUBLANES
        across = [hop(side, 'x', way)
                  for side, way in ((from_sides[0][:cut], RIGHT), (from_sides[1][cut:], LEFT))]

        bias_row = b_head[np.newaxis]
        bias_pad = jnp.concatenate([b_head, jnp.full((RING * SLICE - vocab,), NEG, F32)])
        bias_mine = lax.dynamic_slice_in_dim(bias_pad, lax.axis_index('x') * SLICE, SLICE, ZERO)
        bias_cols = jnp.broadcast_to(bias_mine[:, np.newaxis], (SLICE, LANES)).reshape(-1, PIECE, LANES)
        partial = head_lse(final_bf, w_t, bias_row)
        stats = head_lse(final_bf, w_t, bias_row, partial)
        *gathered, count, log_norm = head_gw(stats, [packet, *from_sides, *across], w_t, bias_cols)
        scale = 1.0 / count[0, :1]

        last = [ORDERS[order][-1] for *_, order, _ in PARTS]
        ways = [way for *_, way in PARTS]
        from_left = [hop(g, a, RIGHT) for g, a in zip(gathered, last)]
        from_right = [hop(g, a, LEFT) for g, a in zip(gathered, last)]
        far = [hop((from_left, from_right)[way][n], a, (RIGHT, LEFT)[way]) for n, (way, a) in enumerate(zip(ways, last))]

        final_bf, _ = lax.optimization_barrier((final_bf, count))
        own_mask = mask_f[0][:, np.newaxis] > ZERO
        own_tag = labels[0][:, np.newaxis] - tp * vocab
        wide = lambda column: jnp.broadcast_to(column, (tokens, LANES))
        lse_b = wide(jnp.where(own_mask, log_norm.reshape(tokens, ONE), -NEG))
        tag_b = wide(jnp.where(own_mask & (own_tag < vocab), own_tag, -ONE))
        grad_final, target, grad_b_head = head_gz(final_bf, w_t, bias_row, lse_b, tag_b)
        hits = jnp.sum(target).reshape(ONE, ONE)
        loss_part = jnp.sum(mask_f * log_norm) - (hits + swap(hits))
        grad_final = grad_final + swap(grad_final)

        grad_resid, grad_lnf_gain, grad_lnf_bias = norm_backward(grad_final, fin_hat, fin_inv, lnf_gain)
        grad_b_fc_out = jnp.sum(grad_resid, axis=ZERO)
        grad_block = grad_resid.astype(BF16)
        grad_context = dot(grad_block, wo, NT).astype(BF16)
        grad_q, grad_k, grad_v = attn_bwd(qs, k_rot, v_proj, grad_context, lse_att, *tables, score_scale)
        grad_pre, = gelu_vjp(dot(grad_block, w_fc_out, NT))
        grad_b_fc_in = jnp.sum(grad_pre, axis=ZERO)
        grad_pre = grad_pre.astype(BF16)
        grad_normed = dot(grad_q, wq, NN) + dot(grad_k, wk, NN) + dot(grad_v, wv, NN) + dot(grad_pre, w_fc_in, NT)
        grad_normed = grad_normed + swap(grad_normed)
        grad_ln_in, grad_ln_gain, grad_ln_bias = norm_backward(grad_normed, ln_hat, ln_inv, ln_gain)
        grad_hidden = ((grad_resid + grad_ln_in) * scale).astype(BF16)

        vectors = [grad_ln_gain, grad_ln_bias, grad_b_fc_in, grad_b_fc_out, grad_lnf_gain, grad_lnf_bias,
                   jnp.broadcast_to(loss_part[0], (dim,)), jnp.sum(grad_b_head, axis=ZERO)]
        ends = list(np.cumsum([v.shape[0] for v in vectors]))
        vectors.append(jnp.zeros((BLOCK[1][0] * RING ** 3 * dim - int(ends[-1]),), F32))
        cube = lambda value, n: value.reshape(-1, RING, RING, BLOCK[n][0], dim)
        first = [cube(dot(g, h, TN), 0) for g, h in ((grad_q, normed), (grad_k, normed), (grad_v, normed), (context, grad_block))]
        sums = chip_sum((first, [cube(jnp.concatenate(vectors), 1)], [cube(dot(gelu_bf, grad_block, TN), 2)],
                         [cube(dot(normed, grad_pre[:, cols], TN), 3) for cols in chunks(grad_pre.shape[-1], dim)]))
        weights, small, fc_out, fc_in = (s.reshape(-1, dim) * scale for s in sums)
        pieces = [small.reshape(-1)[end - v.shape[0]:end] for v, end in zip(vectors, ends)]
        back = lambda n: jnp.moveaxis(weights[n * lanes:(n + ONE) * lanes].reshape(heads, head_dim, dim), -ONE, ZERO)

        coords = jnp.stack([lax.axis_index(a) for a in DP]).astype(jnp.int32)
        grad_w_head = place([(0, dict(enumerate(gathered)))], scale, coords, vocab)
        grad_w_head = place([(3, dict(enumerate(from_left))), (1, dict(enumerate(from_right)))], scale, coords, vocab, grad_w_head)
        grad_w_head = place([(2, dict(enumerate(far)))], scale, coords, vocab, grad_w_head)
        gains = pieces[:2], pieces[2], pieces[3:6]
        return (pieces[6][0], grad_hidden[np.newaxis], *gains[0], back(0), back(1), back(2),
                weights[3 * lanes:].reshape(heads, head_dim, dim), jnp.concatenate([fc_in[:dim], fc_in[dim:]], axis=ONE),
                gains[1], fc_out, *gains[2], grad_w_head.T, pieces[7][:vocab])

    return jax.shard_map(local_step, mesh=mesh, in_specs=DATA_SPECS + PARAM_SPECS,
                         out_specs=(P(), P(DP, None, None)) + PARAM_SPECS, check_vma=False)
```

time: 1170 us -> 744 us (0.64)
  blocking collectives: 541 us -> 0 us
  Pallas kernels: 0 us -> 481 us
  matrix products: 252 us -> 35.6 us
  other arithmetic: 127 us -> 30.9 us
  local copies, waits for them, and re-layouts: 68.6 us -> 26.2 us
  starting transfers between devices: 0.16 us -> 31.4 us
  waiting for transfers between devices: 156 us -> 125 us
    psum x4 -> x0, blocking collectives: 539 us -> none  [the longest x1 353 us: local_step(): lax.psum((loss_part, grad_ln_gain, grad_ln_bias, grad_w_query, grad_w_key...]
    pallas_call x0 -> x10, Pallas kernels: none -> 481 us  [the longest x1 170 us: head_gw(): pl.pallas_call(kernel, in_specs=[WHOLE] + [ANY] * len(packets) + [ANY, WH...]
    dot_general x20 -> x16, matrix products: 235 us -> 35.6 us  [dot(): return lax.dot_general(a, b, dims, preferred_element_type=F32)]
    psum x4 -> x0, waiting for transfers between devices: 156 us -> none  [the longest x1 137 us: local_step(): lax.psum((loss_part, grad_ln_gain, grad_ln_bias, grad_w_query, grad_w_key...]
    ppermute x0 -> x26, waiting for transfers between devices: none -> 125 us  [the longest x22 122 us: hop(): return lax.ppermute(value, axis, way)]
    reduce_sum x11 -> x10, other arithmetic: 110 us -> 18.1 us  [the longest x1 4.8 us: norm_backward(): mean_proj = jnp.mean(grad_hat * x_hat, axis=-ONE, keepdims=True)]
    unnamed x132, local copies, waits for them, and re-layouts: 52.6 us -> 6.51 us
    ppermute x0 -> x26, starting transfers between devices: none -> 31.4 us  [the longest x22 31.4 us: hop(): return lax.ppermute(value, axis, way)]
  transfers between devices with their start and end apart: 4 -> 26, of which waited for: 2 -> 7; matrix products, arithmetic and copies ran while one was open for 6% -> 9% of each run, Pallas kernels for 0% -> 29%
where the time goes in v1:
time: 744 us; the launch traced here: 734 us
  Pallas kernels  481 us (65%)
  waiting for transfers between devices  125 us (17%)
  matrix products  35.6 us (5%)
  starting transfers between devices  31.4 us (4%)
  other arithmetic  30.9 us (4%)
  local copies, waits for them, and re-layouts  26.2 us (4%)
    pallas_call x1, Pallas kernels, head_gw(): pl.pallas_call(kernel, in_specs=[WHOLE] + [ANY] * len(packets) + [ANY, WH...  170 us
    ppermute x22, waiting for transfers between devices, hop(): return lax.ppermute(value, axis, way)  122 us
    pallas_call x1, Pallas kernels, chip_sum(): pl.pallas_call(kernel, in_specs=[ANY] * len(flat), out_specs=[WHOLE] * co...  116 us
    pallas_call x1, Pallas kernels, head_gz(): pl.pallas_call(kernel, grid=(steps,), in_specs=[pl.BlockSpec((tokens, dim...  71.8 us
    pallas_call x3, Pallas kernels, place(): pl.pallas_call(kernel, grid=(steps,), in_specs=[SCALARS, SCALARS, *blocks...  55 us
    pallas_call x2, Pallas kernels, head_lse(): pl.pallas_call(kernel, grid=(early if first else steps - early,), in_spec...  41.9 us
    dot_general x16, matrix products, dot(): return lax.dot_general(a, b, dims, preferred_element_type=F32)  35.6 us
    ppermute x22, starting transfers between devices, hop(): return lax.ppermute(value, axis, way)  31.4 us
  transfers between devices with their start and end apart: 26, of which 7 were waited for; matrix products, arithmetic and copies ran while one was open for 9% of the time, Pallas kernels for 29%

profile of v1, /device:TPU:0, one launch (start us, length us, event | category | flops | bytes accessed | tf_op | source)
XLA Modules:
  0.0 734.5 jit_solution(15737592803902750077)
XLA Ops:
  5.1 3.9 multiply_convert_fusion
  9.1 2.6 fusion.44
  11.6 12.9 %attn_fwd.1 = (bf16[1024,256]{1,0:T(8,128)(2,1)}, bf16[1024,256]{1,0:T(8,128)(2,1)}, bf16[1024,256]{1,0:T(8,128)(2,1)}, bf16[1024,256]{1,0:T(8,128)(2,1)}, f32[2,2,1024]{2,1,0:T(2,128)}) custom-call(bf16[1024,512]{1,0:T(8,128)(2,1)} %copy-done.21, bf16[256,512]{1,0:T(8,128)(2,1)} %bitcast.181, bf16[256,512]{1,0:T(8,128)(2,1)} %bitcast.183, ...), custom_call_target="tpu_custom_call" | custom-call | flops 12999999488 | bytes 1 | tf_op jit(solution)/shard_map/attn_fwd/pallas_call | solution.py:222
  24.5 3.6 convolution_add_fusion
  29.8 2.8 collective-permute-done
  32.6 2.6 fusion.38
  37.7 2.9 collective-permute-start.2
  40.8 20.5 %head_lse_first.1 = (f32[1024,128]{1,0:T(8,128)}, f32[1024,128]{1,0:T(8,128)}) custom-call(bf16[1024,512]{1,0:T(8,128)(2,1)} %get-tuple-element.49.z_ref, bf16[25152,512]{1,0:T(8,128)(2,1)} %bitcast.194, f32[1,25152]{1,0:T(1,128)} %broadcast_in_dim.28.b_ref), custom_call_target="tpu_custom_call" | custom-call | flops 19000000512 | bytes 1 | tf_op jit(solution)/shard_map/head_lse_first/pallas_call | solution.py:123
  61.2 2.4 collective-permute-done.2.refs_2_
  63.7 3.8 collective-permute-start.4
  68.7 21.5 %head_lse_rest.1.stats_ref = f32[2,1024]{1,0:T(2,128)} custom-call(bf16[1024,512]{1,0:T(8,128)(2,1)} %get-tuple-element.49.z_ref, bf16[25152,512]{1,0:T(8,128)(2,1)} %bitcast.195, f32[1,25152]{1,0:T(1,128)} %broadcast_in_dim.28.b_ref, f32[1024,128]{1,0:T(8,128)} %get-tuple-element.46.refs_0_, f32[1024,128]{1,0:T(8,128)} %get-tuple-element.47.refs_1_), custom_call_target="tpu_custom_call" | custom-call | flops 19000000512 | bytes 1 | tf_op jit(solution)/shard_map/head_lse_rest/pallas_call | solution.py:123
  92.4 170.2 %head_gw.1 = (f32[4,4,72,512]{3,2,1,0:T(8,128)}, f32[4,4,64,512]{3,2,1,0:T(8,128)}, f32[4,4,64,512]{3,2,1,0:T(8,128)}, f32[4,4,64,512]{3,2,1,0:T(8,128)}, f32[4,...) custom-call(f32[2,1024]{1,0:T(2,128)} %head_lse_rest.1.stats_ref, ...), custom_call_target="tpu_custom_call" | custom-call | flops 160000000000 | bytes 1 | tf_op jit(solution)/shard_map/head_gw/pallas_call | solution.py:542
  265.3 71.8 %head_gz.1 = (f32[1024,512]{1,0:T(8,128)}, f32[1024,128]{1,0:T(8,128)}, f32[8,25600]{1,0:T(8,128)}) custom-call(bf16[1024,512]{1,0:T(8,128)(2,1)} %get-tuple-element.49.z_ref, bf16[25152,512]{1,0:T(8,128)(2,1)} %bitcast.197, f32[1,25152]{1,0:T(1,128)} %broadcast_in_dim.28.b_ref, f32[1024,128]{1,0:T(8,128)} %broadcast_in_dim.33.lse_ref, ...), custom_call_target="tpu_custom_call" | custom-call | flops 71999995904 | bytes 1 | tf_op jit(solution)/shard_map/head_gz/pallas_call | solution.py:174
  342.0 3.0 collective-permute-start.14
  346.5 16.0 %shard_map.306.refs_12_ = f32[25152,512]{1,0:T(8,128)} custom-call(s32[3]{0:T(128)} %pad_add_fusion.coord_ref, f32[1]{0:T(128)} %bitcast.61.scale_ref, f32[4,4,72,512]{3,2,1,0:T(8,128)} %get-tuple-element.62.refs_0_, f32[4,4,64,512]{3,2,1,0:T(8,128)} %get-tuple-element.63.refs_1_, f32[4,4,64,512]{3,2,1,0:T(8,128)} %get-tuple-element.64.refs_2_, ...), custom_call_target="tpu_custom_call" | custom-call | flops 12000000000 | bytes 1 | tf_op jit(solution)/shard_map/pallas_call | solution.py:672
  367.6 3.4 multiply_reduce_fusion
  374.3 14.8 %collective-permute-done.10.refs_7_ = f32[4,4,64,512]{3,2,1,0:T(8,128)} collective-permute-done((f32[4,4,64,512]{3,2,1,0:T(8,128)}, f32[4,4,64,512]{3,2,1,0:T(8,128)}, u32[]{:S(2)}, u32[]{:S(2)}) %collective-permute-start.10) | collective-permute-done | bytes 2097184 | tf_op jit(solution)/shard_map/ppermute | solution.py:706
  392.3 12.8 %attn_bwd.1 = (bf16[1024,256]{1,0:T(8,128)(2,1)}, bf16[1024,256]{1,0:T(8,128)(2,1)}, bf16[1024,256]{1,0:T(8,128)(2,1)}) custom-call(bf16[1024,256]{1,0:T(8,128)(2,1)} %get-tuple-element.42.qs_ref, bf16[1024,256]{1,0:T(8,128)(2,1)} %get-tuple-element.43.k_ref, bf16[1024,256]{1,0:T(8,128)(2,1)} %get-tuple-element.44.v_ref, ...), custom_call_target="tpu_custom_call" | custom-call | flops 12999999488 | bytes 1 | tf_op jit(solution)/shard_map/attn_bwd/pallas_call | solution.py:263
  409.3 2.7 convolution_bitcast_fusion.refs_2_
  415.0 5.0 fusion.40
  424.2 13.5 %collective-permute-done.21.refs_3_ = f32[4,4,64,512]{3,2,1,0:T(8,128)} collective-permute-done((f32[4,4,64,512]{3,2,1,0:T(8,128)}, f32[4,4,64,512]{3,2,1,0:T(8,128)}, u32[]{:S(2)}, u32[]{:S(2)}) %collective-permute-start.21) | collective-permute-done | bytes 2097184 | tf_op jit(solution)/shard_map/ppermute | solution.py:706
  441.4 3.1 collective-permute-start.25
  444.6 2.6 convolution_bitcast_fusion.2.refs_0_
  453.5 2.6 fusion.49
  457.9 59.6 %collective-permute-done.25.refs_10_ = f32[4,4,64,512]{3,2,1,0:T(8,128)} collective-permute-done((f32[4,4,64,512]{3,2,1,0:T(8,128)}, f32[4,4,64,512]{3,2,1,0:T(8,128)}, u32[]{:S(2)}, u32[]{:S(2)}) %collective-permute-start.25) | collective-permute-done | bytes 2097184 | tf_op jit(solution)/shard_map/ppermute | solution.py:706
  519.7 3.2 collective-permute-start.15
  522.9 3.1 collective-permute-start.19
  525.9 23.2 %shard_map.307.refs_6_ = f32[25152,512]{1,0:T(8,128)} custom-call(s32[3]{0:T(128)} %pad_add_fusion.coord_ref, f32[1]{0:T(128)} %bitcast.61.scale_ref, f32[4,4,72,512]{3,2,1,0:T(8,128)} %collective-permute-done.8.refs_0_, f32[4,4,64,512]{3,2,1,0:T(8,128)} %collective-permute-done.20.refs_1_, ...), custom_call_target="tpu_custom_call", output_to_operand_aliasing={{}: (14, {})} | custom-call | flops 24000000000 | bytes 1 | tf_op jit(solution)/shard_map/pallas_call | solution.py:672
  549.2 4.8 fusion.17
  555.3 116.0 %chip_sum.1 = (f32[4,4,4,16,512]{4,3,2,1,0:T(8,128)}, f32[4,4,4,8,512]{4,3,2,1,0:T(8,128)}, f32[4,4,4,16,512]{4,3,2,1,0:T(8,128)}, f32[4,4,4,16,512]{4,3,2,1,0:T(8,128)}) custom-call(f32[1,4,4,16,512]{4,3,2,1,0:T(8,128)} %convolution_bitcast_fusion.2.refs_0_, f32[1,4,4,16,512]{4,3,2,1,0:T(8,128)} %convolution_bitcast_fusion.1.refs_1_, ...), custom_call_target="tpu_custom_call" | custom-call | flops 60000002048 | bytes 1 | tf_op jit(solution)/shard_map/chip_sum/pallas_call | solution.py:621
  687.0 31.2 %collective-permute-done.17.refs_4_ = f32[4,4,64,512]{3,2,1,0:T(8,128)} collective-permute-done((f32[4,4,64,512]{3,2,1,0:T(8,128)}, f32[4,4,64,512]{3,2,1,0:T(8,128)}, u32[]{:S(2)}, u32[]{:S(2)}) %collective-permute-start.17) | collective-permute-done | bytes 2097184 | tf_op jit(solution)/shard_map/ppermute | solution.py:706
  718.2 15.8 %shard_map.308 = f32[25152,512]{1,0:T(8,128)} custom-call(s32[3]{0:T(128)} %pad_add_fusion.coord_ref, f32[1]{0:T(128)} %bitcast.61.scale_ref, f32[4,4,72,512]{3,2,1,0:T(8,128)} %collective-permute-done.9.refs_0_, f32[4,4,64,512]{3,2,1,0:T(8,128)} %collective-permute-done.11.refs_1_, ...), custom_call_target="tpu_custom_call", output_to_operand_aliasing={{}: (8, {})} | custom-call | flops 12000000000 | bytes 1 | tf_op jit(solution)/shard_map/pallas_call | solution.py:672
  (240 shorter events, 72.2 us)
Async XLA Ops:
  28.1 4.5 collective-permute-start
  37.7 26.0 %collective-permute-start.2 = (f32[520,512]{1,0:T(8,128)S(1)}, f32[520,512]{1,0:T(8,128)S(1)}, u32[]{:S(2)}, u32[]{:S(2)}) collective-permute-start(f32[520,512]{1,0:T(8,128)S(1)} %maximum_maximum_fusion.refs_0_), channel_id=1, source_target_pairs={{0,3},{1,0},{2,1},{3,2},{4,7},{5,4},{6,5},{7,6},{8,11},{9,8},{10,9... | collective-permute-start | bytes 3194888 | tf_op jit(solution)/shard_map/ppermute | solution.py:706
  40.6 26.9 %collective-permute-start.1 = (f32[520,512]{1,0:T(8,128)S(1)}, f32[520,512]{1,0:T(8,128)}, u32[]{:S(2)}, u32[]{:S(2)}) collective-permute-start(f32[520,512]{1,0:T(8,128)S(1)} %maximum_maximum_fusion.refs_0_), channel_id=1, source_target_pairs={{0,1},{1,2},{2,3},{3,0},{4,5},{5,6},{6,7},{7,4},{8,9},{9,10},{10,1... | collective-permute-start | bytes 3194888 | tf_op jit(solution)/shard_map/ppermute | solution.py:706
  63.7 26.4 %collective-permute-start.4 = (f32[264,512]{1,0:T(8,128)S(1)}, f32[264,512]{1,0:T(8,128)}, u32[]{:S(2)}, u32[]{:S(2)}) collective-permute-start(f32[264,512]{1,0:T(8,128)S(1)} %slice.125), channel_id=1, source_target_pairs={{0,3},{1,0},{2,1},{3,2},{4,7},{5,4},{6,5},{7,6},{8,11},{9,8},{10,9... | collective-permute-start | bytes 1622024 | tf_op jit(solution)/shard_map/ppermute | solution.py:706
  68.6 21.6 %collective-permute-start.3 = (f32[256,512]{1,0:T(8,128)S(1)}, f32[256,512]{1,0:T(8,128)S(1)}, u32[]{:S(2)}, u32[]{:S(2)}) collective-permute-start(f32[256,512]{1,0:T(8,128)S(1)} %slice.124), channel_id=1, source_target_pairs={{0,1},{1,2},{2,3},{3,0},{4,5},{5,6},{6,7},{7,4},{8,9},{9,10},{10,1... | collective-permute-start | bytes 1572872 | tf_op jit(solution)/shard_map/ppermute | solution.py:706
  92.4 170.2 %copy-start.47 = (pred[1024]{0:T(1024)(128)(4,1)S(1)}, pred[1024]{0:T(1024)(128)(4,1)}, u32[]{:S(2)}) copy-start(pred[1024]{0:T(1024)(128)(4,1)} %copy-done.46) | copy-start | bytes 3076
  92.4 171.9 %copy-start.43 = (s32[1024]{0:T(1024)S(1)}, s32[1024]{0:T(1024)}, u32[]{:S(2)}) copy-start(s32[1024]{0:T(1024)} %and_select_fusion) | copy-start | bytes 12292
  265.3 71.9 %copy-start.30 = (f32[1024]{0:T(1024)S(1)}, f32[1024]{0:T(1024)}, u32[]{:S(2)}) copy-start(f32[1024]{0:T(1024)} %copy-done.29) | copy-start | bytes 12292
  265.3 71.9 %copy-start.32 = (f32[1024]{0:T(1024)S(1)}, f32[1024]{0:T(1024)}, u32[]{:S(2)}) copy-start(f32[1024]{0:T(1024)} %copy-done.31) | copy-start | bytes 12292
  265.3 71.9 %copy-start.40 = (f32[512]{0:T(512)S(1)}, f32[512]{0:T(512)}, u32[]{:S(2)}) copy-start(f32[512]{0:T(512)} %param.22) | copy-start | bytes 6148
  265.3 71.9 %copy-start.49 = (f32[512]{0:T(512)S(1)}, f32[512]{0:T(512)}, u32[]{:S(2)}) copy-start(f32[512]{0:T(512)} %param.23) | copy-start | bytes 6148
  337.1 29.4 %collective-permute-start.5 = (f32[1024,512]{1,0:T(8,128)}, f32[1024,512]{1,0:T(8,128)}, u32[]{:S(2)}, u32[]{:S(2)}) collective-permute-start(f32[1024,512]{1,0:T(8,128)} %get-tuple-element.51), channel_id=1, source_target_pairs={{0,64},{64,0},{1,65},{65,1},{2,66},{66,2},{3,67},{67,3},{4,68},{68... | collective-permute-start | bytes 6291464 | tf_op jit(solution)/shard_map/ppermute | solution.py:720
  340.8 48.3 %collective-permute-start.10 = (f32[4,4,64,512]{3,2,1,0:T(8,128)}, f32[4,4,64,512]{3,2,1,0:T(8,128)}, u32[]{:S(2)}, u32[]{:S(2)}) collective-permute-start(f32[4,4,64,512]{3,2,1,0:T(8,128)} %get-tuple-element.63.refs_1_), channel_id=1, source_target_pairs={{0,48},{16,0},{32,16},{48,32},{1,49},{17,1},{33,17},{49,33},{2,50}... | collective-permute-start | bytes 6291464 | tf_op jit(solution)/shard_map/ppermute | solution.py:706
  341.8 49.2 %collective-permute-start.12 = (f32[4,4,64,512]{3,2,1,0:T(8,128)}, f32[4,4,64,512]{3,2,1,0:T(8,128)}, u32[]{:S(2)}, u32[]{:S(2)}) collective-permute-start(f32[4,4,64,512]{3,2,1,0:T(8,128)} %get-tuple-element.64.refs_2_), channel_id=1, source_target_pairs={{0,1},{1,2},{2,3},{3,0},{4,5},{5,6},{6,7},{7,4},{8,9},{9,10},{10,1... | collective-permute-start | bytes 6291464 | tf_op jit(solution)/shard_map/ppermute | solution.py:706
  342.0 78.0 %collective-permute-start.14 = (f32[4,4,64,512]{3,2,1,0:T(8,128)}, f32[4,4,64,512]{3,2,1,0:T(8,128)}, u32[]{:S(2)}, u32[]{:S(2)}) collective-permute-start(f32[4,4,64,512]{3,2,1,0:T(8,128)} %get-tuple-element.65.refs_3_), channel_id=1, source_target_pairs={{0,3},{1,0},{2,1},{3,2},{4,7},{5,4},{6,5},{7,6},{8,11},{9,8},{10,9... | collective-permute-start | bytes 6291464 | tf_op jit(solution)/shard_map/ppermute | solution.py:706
  345.7 18.8 %collective-permute-start.7 = (f32[1,1]{1,0:T(1,128)}, f32[1,1]{1,0:T(1,128)}, u32[]{:S(2)}, u32[]{:S(2)}) collective-permute-start(f32[1,1]{1,0:T(1,128)} %bitcast.30), channel_id=1, source_target_pairs={{0,64},{64,0},{1,65},{65,1},{2,66},{66,2},{3,67},{67,3},{4,68},{68... | collective-permute-start | bytes 20 | tf_op jit(solution)/shard_map/ppermute | solution.py:720
  364.5 57.1 %collective-permute-start.16 = (f32[4,4,64,512]{3,2,1,0:T(8,128)}, f32[4,4,64,512]{3,2,1,0:T(8,128)}, u32[]{:S(2)}, u32[]{:S(2)}) collective-permute-start(f32[4,4,64,512]{3,2,1,0:T(8,128)} %get-tuple-element.66.refs_4_), channel_id=1, source_target_pairs={{0,4},{4,8},{8,12},{12,0},{1,5},{5,9},{9,13},{13,1},{2,6},{6,10},{... | collective-permute-start | bytes 6291464 | tf_op jit(solution)/shard_map/ppermute | solution.py:706
  366.4 55.6 %collective-permute-start.20 = (f32[4,4,64,512]{3,2,1,0:T(8,128)}, f32[4,4,64,512]{3,2,1,0:T(8,128)}, u32[]{:S(2)}, u32[]{:S(2)}) collective-permute-start(f32[4,4,64,512]{3,2,1,0:T(8,128)} %get-tuple-element.63.refs_1_), channel_id=1, source_target_pairs={{0,16},{16,32},{32,48},{48,0},{1,17},{17,33},{33,49},{49,1},{2,18}... | collective-permute-start | bytes 6291464 | tf_op jit(solution)/shard_map/ppermute | solution.py:706
  389.1 48.7 %collective-permute-start.21 = (f32[4,4,64,512]{3,2,1,0:T(8,128)}, f32[4,4,64,512]{3,2,1,0:T(8,128)}, u32[]{:S(2)}, u32[]{:S(2)}) collective-permute-start(f32[4,4,64,512]{3,2,1,0:T(8,128)} %get-tuple-element.65.refs_3_), channel_id=1, source_target_pairs={{0,1},{1,2},{2,3},{3,0},{4,5},{5,6},{6,7},{7,4},{8,9},{9,10},{10,1... | collective-permute-start | bytes 6291464 | tf_op jit(solution)/shard_map/ppermute | solution.py:706
  391.0 50.4 %collective-permute-start.24 = (f32[4,4,64,512]{3,2,1,0:T(8,128)}, f32[4,4,64,512]{3,2,1,0:T(8,128)}, u32[]{:S(2)}, u32[]{:S(2)}) collective-permute-start(f32[4,4,64,512]{3,2,1,0:T(8,128)} %get-tuple-element.64.refs_2_), channel_id=1, source_target_pairs={{0,3},{1,0},{2,1},{3,2},{4,7},{5,4},{6,5},{7,6},{8,11},{9,8},{10,9... | collective-permute-start | bytes 6291464 | tf_op jit(solution)/shard_map/ppermute | solution.py:706
  420.0 97.5 %collective-permute-start.18 = (f32[4,4,72,512]{3,2,1,0:T(8,128)}, f32[4,4,72,512]{3,2,1,0:T(8,128)}, u32[]{:S(2)}, u32[]{:S(2)}) collective-permute-start(f32[4,4,72,512]{3,2,1,0:T(8,128)} %get-tuple-element.67.refs_5_), channel_id=1, source_target_pairs={{0,12},{4,0},{8,4},{12,8},{1,13},{5,1},{9,5},{13,9},{2,14},{6,2},{... | collective-permute-start | bytes 7077896 | tf_op jit(solution)/shard_map/ppermute | solution.py:706
  421.6 98.0 %collective-permute-start.22 = (f32[4,4,72,512]{3,2,1,0:T(8,128)}, f32[4,4,72,512]{3,2,1,0:T(8,128)}, u32[]{:S(2)}, u32[]{:S(2)}) collective-permute-start(f32[4,4,72,512]{3,2,1,0:T(8,128)} %get-tuple-element.67.refs_5_), channel_id=1, source_target_pairs={{0,4},{4,8},{8,12},{12,0},{1,5},{5,9},{9,13},{13,1},{2,6},{6,10},{... | collective-permute-start | bytes 7077896 | tf_op jit(solution)/shard_map/ppermute | solution.py:706
  422.0 97.6 %collective-permute-start.23 = (f32[4,4,72,512]{3,2,1,0:T(8,128)}, f32[4,4,72,512]{3,2,1,0:T(8,128)}, u32[]{:S(2)}, u32[]{:S(2)}) collective-permute-start(f32[4,4,72,512]{3,2,1,0:T(8,128)} %get-tuple-element.62.refs_0_), channel_id=1, source_target_pairs={{0,48},{16,0},{32,16},{48,32},{1,49},{17,1},{33,17},{49,33},{2,50}... | collective-permute-start | bytes 7077896 | tf_op jit(solution)/shard_map/ppermute | solution.py:706
  437.7 85.2 %collective-permute-start.8 = (f32[4,4,72,512]{3,2,1,0:T(8,128)}, f32[4,4,72,512]{3,2,1,0:T(8,128)}, u32[]{:S(2)}, u32[]{:S(2)}) collective-permute-start(f32[4,4,72,512]{3,2,1,0:T(8,128)} %get-tuple-element.62.refs_0_), channel_id=1, source_target_pairs={{0,16},{16,32},{32,48},{48,0},{1,17},{17,33},{33,49},{49,1},{2,18}... | collective-permute-start | bytes 7077896 | tf_op jit(solution)/shard_map/ppermute | solution.py:706
  441.4 76.0 %collective-permute-start.25 = (f32[4,4,64,512]{3,2,1,0:T(8,128)}, f32[4,4,64,512]{3,2,1,0:T(8,128)}, u32[]{:S(2)}, u32[]{:S(2)}) collective-permute-start(f32[4,4,64,512]{3,2,1,0:T(8,128)} %get-tuple-element.66.refs_4_), channel_id=1, source_target_pairs={{0,12},{4,0},{8,4},{12,8},{1,13},{5,1},{9,5},{13,9},{2,14},{6,2},{... | collective-permute-start | bytes 6291464 | tf_op jit(solution)/shard_map/ppermute | solution.py:706
  517.4 31.7 %collective-permute-start.6 = (f32[1024,512]{1,0:T(8,128)}, f32[1024,512]{1,0:T(8,128)}, u32[]{:S(2)}, u32[]{:S(2)}) collective-permute-start(f32[1024,512]{1,0:T(8,128)} %add_add_fusion), channel_id=1, source_target_pairs={{0,64},{64,0},{1,65},{65,1},{2,66},{66,2},{3,67},{67,3},{4,68},{68... | collective-permute-start | bytes 6291464 | tf_op jit(solution)/shard_map/ppermute | solution.py:720
  517.4 159.1 %collective-permute-start.11 = (f32[4,4,64,512]{3,2,1,0:T(8,128)}, f32[4,4,64,512]{3,2,1,0:T(8,128)}, u32[]{:S(2)}, u32[]{:S(2)}) collective-permute-start(f32[4,4,64,512]{3,2,1,0:T(8,128)} %collective-permute-done.10.refs_7_), channel_id=1, source_target_pairs={{0,48},{16,0},{32,16},{48,32},{1,49},{17,1},{33,17},{49,33},{2,50}... | collective-permute-start | bytes 6291464 | tf_op jit(solution)/shard_map/ppermute | solution.py:706
  519.6 167.4 %collective-permute-start.13 = (f32[4,4,64,512]{3,2,1,0:T(8,128)}, f32[4,4,64,512]{3,2,1,0:T(8,128)}, u32[]{:S(2)}, u32[]{:S(2)}) collective-permute-start(f32[4,4,64,512]{3,2,1,0:T(8,128)} %collective-permute-done.12.refs_2_), channel_id=1, source_target_pairs={{0,1},{1,2},{2,3},{3,0},{4,5},{5,6},{6,7},{7,4},{8,9},{9,10},{10,1... | collective-permute-start | bytes 6291464 | tf_op jit(solution)/shard_map/ppermute | solution.py:706
  519.7 167.4 %collective-permute-start.15 = (f32[4,4,64,512]{3,2,1,0:T(8,128)}, f32[4,4,64,512]{3,2,1,0:T(8,128)}, u32[]{:S(2)}, u32[]{:S(2)}) collective-permute-start(f32[4,4,64,512]{3,2,1,0:T(8,128)} %collective-permute-done.14.refs_9_), channel_id=1, source_target_pairs={{0,3},{1,0},{2,1},{3,2},{4,7},{5,4},{6,5},{7,6},{8,11},{9,8},{10,9... | collective-permute-start | bytes 6291464 | tf_op jit(solution)/shard_map/ppermute | solution.py:706
  522.9 195.3 %collective-permute-start.19 = (f32[4,4,72,512]{3,2,1,0:T(8,128)}, f32[4,4,72,512]{3,2,1,0:T(8,128)}, u32[]{:S(2)}, u32[]{:S(2)}) collective-permute-start(f32[4,4,72,512]{3,2,1,0:T(8,128)} %collective-permute-done.18.refs_11_), channel_id=1, source_target_pairs={{0,12},{4,0},{8,4},{12,8},{1,13},{5,1},{9,5},{13,9},{2,14},{6,2},{... | collective-permute-start | bytes 7077896 | tf_op jit(solution)/shard_map/ppermute | solution.py:706
  549.2 169.1 %collective-permute-start.9 = (f32[4,4,72,512]{3,2,1,0:T(8,128)}, f32[4,4,72,512]{3,2,1,0:T(8,128)}, u32[]{:S(2)}, u32[]{:S(2)}) collective-permute-start(f32[4,4,72,512]{3,2,1,0:T(8,128)} %collective-permute-done.8.refs_0_), channel_id=1, source_target_pairs={{0,16},{16,32},{32,48},{48,0},{1,17},{17,33},{33,49},{49,1},{2,18}... | collective-permute-start | bytes 7077896 | tf_op jit(solution)/shard_map/ppermute | solution.py:706
  676.6 41.6 %collective-permute-start.17 = (f32[4,4,64,512]{3,2,1,0:T(8,128)}, f32[4,4,64,512]{3,2,1,0:T(8,128)}, u32[]{:S(2)}, u32[]{:S(2)}) collective-permute-start(f32[4,4,64,512]{3,2,1,0:T(8,128)} %collective-permute-done.16.refs_4_), channel_id=1, source_target_pairs={{0,4},{4,8},{8,12},{12,0},{1,5},{5,9},{9,13},{13,1},{2,6},{6,10},{... | collective-permute-start | bytes 6291464 | tf_op jit(solution)/shard_map/ppermute | solution.py:706
  (55 other events, 422.5 us)

commit v2 on v1

--- a/solution.py
+++ b/solution.py
@@ -1,4 +1,5 @@
 import functools
+import itertools
 import jax
 import jax.numpy as jnp
 import numpy as np
@@ -31,7 +32,9 @@
 SLICE = TWO * HALF_SLICE
 ORDERS = (('x', 'y', 'z'), ('y', 'z', 'x'), ('z', 'x', 'y'))
 PARTS = ((72, 0, 0, 0, 0), (64, 72, 0, 0, 1), (64, 136, 0, 1, 0), (64, 0, 1, 1, 1), (64, 64, 1, 2, 0), (72, 128, 1, 2, 1))
-BLOCK = ((16, 0), (8, 0), (16, 1), (16, 2))
+BLOCK = (0, 1, 2, 0, 1, 2)
+ROWS = 8
+FEW = 16
 HALVES = (pl.ds(0, 2), pl.ds(2, 2))
 MESH_ID = pl.DeviceIdType.MESH
 ANY, WHOLE, SCALARS = (pl.BlockSpec(memory_space=space) for space in (pl.ANY, pltpu.VMEM, pltpu.SMEM))
@@ -81,7 +84,7 @@
     tokens, dim = z.shape
     vocab = w_t.shape[0]
     steps = pl.cdiv(vocab, tile)
-    early = steps // TWO
+    early = steps * 3 // 5
     offset = ZERO if begin is None else early
 
     def kernel(z_ref, w_ref, b_ref, *refs):
@@ -129,56 +132,6 @@
         scratch_shapes=[] if first else [pltpu.VMEM((tokens, LANES), F32)] * TWO,
         compiler_params=params(), cost_estimate=cost(19), name='head_lse_first' if first else 'head_lse_rest',
     )(z, w_t, bias, *(begin or ()))
-
-
-def head_gz(z, w_t, bias, lse, tag, tile=2560, sub=2560):
-    tokens, dim = z.shape
-    vocab = w_t.shape[0]
-    steps = pl.cdiv(vocab, tile)
-
-    def kernel(z_ref, w_ref, b_ref, lse_ref, tag_ref, gz_ref, t_ref, gb_ref):
-        step = pl.program_id(ZERO)
-
-        @pl.when(step == ZERO)
-        def _():
-            gz_ref[...] = jnp.zeros_like(gz_ref)
-            t_ref[...] = jnp.zeros_like(t_ref)
-
-        def work(last):
-            zz = z_ref[...]
-            lane = iota((tokens, LANES), ONE)
-            for part in chunks(tile, sub):
-                w = w_ref[part, :]
-                left = vocab - step * tile - part.start
-                if last:
-                    w = jnp.where(iota(w.shape, ZERO) < left, w, jnp.zeros_like(w))
-                l = dot(zz, w, NT) + b_ref[:, part]
-                norm, rel = lse_ref[...], tag_ref[...] - (step * tile + part.start)
-                grads, targets = [], []
-                for c in chunks(sub):
-                    hit = lane == rel - c.start
-                    prob = jnp.exp(l[:, c] - norm)
-                    if last:
-                        prob = jnp.where(lane < left - c.start, prob, 0.0)
-                    grads.append(prob - jnp.where(hit, 1.0, 0.0))
-                    targets.append(jnp.where(hit, l[:, c], 0.0))
-                t_ref[...] += sum(targets)
-                grad = jnp.concatenate(grads, axis=ONE)
-                gb_ref[:, part] = jnp.sum(grad.reshape(-1, SUBLANES, sub), axis=ZERO)
-                gz_ref[...] += dot(grad.astype(BF16), w, NN)
-
-        pl.when(step < steps - ONE)(lambda: work(last=False))
-        pl.when(step == steps - ONE)(lambda: work(last=True))
-
-    narrow = pl.BlockSpec((tokens, LANES), origin)
-    return pl.pallas_call(
-        kernel, grid=(steps,),
-        in_specs=[pl.BlockSpec((tokens, dim), origin), pl.BlockSpec((tile, dim), row_block), pl.BlockSpec((ONE, tile), column_block),
-                  narrow, narrow],
-        out_specs=[pl.BlockSpec((tokens, dim), origin), narrow, pl.BlockSpec((SUBLANES, tile), column_block)],
-        out_shape=[struct((tokens, dim)), struct((tokens, LANES)), struct((SUBLANES, steps * tile))],
-        compiler_params=params(), cost_estimate=cost(72), name='head_gz',
-    )(z, w_t, bias, lse, tag)
 
 
 def swap_pairs(x, even):
@@ -317,10 +270,10 @@
         self.plain, self.added = ([wires.line(functools.partial(sent, part, s, turn), functools.partial(kept, part, s), axis, turn)
                                    for s, turn in enumerate(TURNS)] for part in (halves[::-1], halves))
 
-    def relay(self):
-        for s, turn in enumerate(TURNS):
+    def relay(self, sides=range(TWO)):
+        for s in sides:
             arrive([self.first[s]])
-            part = self.piece(turn).at[self.halves[s]]
+            part = self.piece(TURNS[s]).at[self.halves[s]]
             part[...] = part[...] + self.near[s][...]
             start([self.added[s]])
 
@@ -338,6 +291,18 @@
     def result(self):
         arrive(self.lines)
         return self.piece(ZERO)[...] + (self.landing[0] + self.landing[1] + self.landing[2])
+
+
+class FanAll:
+    def __init__(self, wires, axis, value, landing):
+        self.value, self.landing, mine = value, landing, lax.axis_index(axis)
+        self.lines = [wires.line(lambda: value, lambda: landing.at[mine], axis, turn) for turn in range(ONE, RING)]
+        self.mine = mine
+
+    def result(self):
+        self.landing[self.mine] = self.value[...]
+        arrive(self.lines)
+        return self.landing[0] + self.landing[1] + (self.landing[2] + self.landing[3])
 
 
 class RingGather:
@@ -350,7 +315,7 @@
             self.relays.append((way, wires.line(passed, passed, axis, TURNS[way])))
         self.idle = [s for s in range(TWO) if s not in dict(relays)]
 
-    def forward(self):
+    def relay(self):
         for way, line in self.relays:
             arrive([self.step[way]])
             start([line])
@@ -373,43 +338,63 @@
     return at, lambda axis, turn: lax.rem(at[axis] + turn, RING)
 
 
-def head_gw(stats, packets, w_t, bias_cols):
+def head_grads(stats, packets, w_t, bias_cols, bias_row, tile=1280):
     tokens = stats.shape[1]
     dim = w_t.shape[1]
     vocab = w_t.shape[0]
+    tiles = bias_row.shape[1] // tile
     half = tokens // TWO
+    block = PIECE // TWO
     low = 104
     halves = (pl.ds(ZERO, low), pl.ds(low, UNIT - low))
     colors = (('y', 'z'), ('z', 'y'))
     group = [(x, c) for c in range(TWO) for x in range(RING)][1:]
     firsts = [ZERO] * RING + [packets[3].shape[0]]
+    n_packets, n_parts = len(packets), len(PARTS)
 
     def spot(ref, n):
         return ref.at[min(n, 3), pl.ds(firsts[n], packets[n].shape[0])]
 
     def kernel(stats_ref, *refs):
-        packet_refs, (w_ref, bias_ref), refs = refs[:len(packets)], refs[len(packets):len(packets) + TWO], refs[len(packets) + TWO:]
-        outs, (count_out, norm_out), refs = refs[:len(PARTS)], refs[len(PARTS):len(PARTS) + TWO], refs[len(PARTS) + TWO:]
-        (acc, w_all, zb, own, theirs, heard, norms, tags, shard, tally, *lanes, send, recv, local) = refs
+        packet_refs, (w_ref, cols_ref, bias_ref), refs = refs[:n_packets], refs[n_packets:n_packets + 3], refs[n_packets + 3:]
+        outs, (count_out, norm_out, gz_ref, t_ref, gb_ref), refs = refs[:n_parts], refs[n_parts:n_parts + 5], refs[n_parts + 5:]
+        (acc, w_bufs, col_bufs, zb, own, theirs, heard, norms, tags, shard, tally, big_w, lse_cols, tag_cols, *lanes, send, recv, local) = refs
         at, beside = coordinates()
         tp = lax.axis_index('tp')
         wires = Wires(send, recv)
 
+        def part_of(h):
+            stage, c, s = lax.div(h, RING), lax.rem(lax.div(h, TWO), TWO), lax.rem(h, TWO)
+            inner = lax.div(stage * (3 - stage), TWO)
+            flip = lax.div(stage * (TWO - stage) * (3 - stage), TWO)
+            ahead = inner * (1 + TWO * s) + TWO * lax.div(3 - stage, 3)
+            return c * RING + lax.rem(at['y'] + (at['z'] - at['y']) * c + ahead, RING), s + flip * (1 - TWO * s)
+
+        def fetch(h, act):
+            p, side = part_of(h)
+            slot = lax.rem(h, TWO)
+            row = pl.multiple_of(at['x'] * SLICE + p * PIECE + side * block, 16)
+            whole = row + block <= vocab
+
+            def move(size):
+                act(pltpu.make_async_copy(w_ref.at[pl.ds(row, size)], w_bufs.at[slot, pl.ds(ZERO, size)], local.at[slot]))
+
+            pl.when(whole)(functools.partial(move, block))
+            pl.when(jnp.logical_and(row < vocab, jnp.logical_not(whole)))(functools.partial(move, vocab % block))
+            act(pltpu.make_async_copy(cols_ref.at[p * TWO + side], col_bufs.at[slot], local.at[TWO + slot]))
+            return p, side, slot, row
+
+        def begin(copy):
+            copy.start()
+
+        def end(copy):
+            copy.wait()
+
         entered = greet([(('x', x), ('tp', c)) for x, c in group] + [((a, t),) for a in ('y', 'z') for t in range(ONE, RING)])
-        loads = [pltpu.make_async_copy(ref, spot(own, n), local.at[n]) for n, ref in enumerate(packet_refs)]
+        fetch(ZERO, begin)
+        loads = [pltpu.make_async_copy(ref, spot(own, n), local.at[RING + n]) for n, ref in enumerate(packet_refs)]
         for load in loads:
             load.start()
-        for n in range(TWO * RING):
-            row = pl.multiple_of(at['x'] * SLICE + n * PIECE, 32)
-            whole = row + PIECE <= vocab
-
-            @pl.when(whole)
-            def _():
-                pltpu.make_async_copy(w_ref.at[pl.ds(row, PIECE)], w_all.at[n], local.at[len(packets) + n]).start()
-
-            @pl.when(jnp.logical_not(whole))
-            def _():
-                pltpu.make_async_copy(w_ref.at[pl.ds(row, vocab % PIECE)], w_all.at[n, pl.ds(ZERO, vocab % PIECE)], local.at[len(packets) + n]).start()
         entered()
         news = []
         for n, (x, c) in enumerate(group):
@@ -418,7 +403,7 @@
             wires.all.append(functools.partial(lambda n: news[n], n))
             news[n].start()
         swaps = [wires.line(functools.partial(lambda n: packet_refs[n], n), functools.partial(spot, theirs, n), 'tp', ONE)
-                 for n in range(len(packets))]
+                 for n in range(n_packets)]
         start(swaps)
         mine = pl.multiple_of(tp * half, half)
         other = pl.multiple_of(half - tp * half, half)
@@ -434,12 +419,15 @@
             top = jnp.maximum(a[0:1], b[0:1])
             norm = top + jnp.log(a[1:2] * jnp.exp(a[0:1] - top) + b[1:2] * jnp.exp(b[0:1] - top))
             label, mask = (jnp.concatenate([own[r, half + n:half + n + ONE] for n in (row, row + ONE)], axis=ONE) for row in (ZERO, TWO))
+            tag = label - (tp * vocab).astype(F32)
             norms[r] = jnp.where(mask > 0.0, norm, -NEG)
-            tags[r] = jnp.where(mask > 0.0, label - (tp * vocab).astype(F32), NEG)
+            tags[r] = jnp.where((mask > 0.0) & (tag < vocab), tag, NEG)
             seen = jnp.broadcast_to(jnp.sum(mask, axis=ONE, keepdims=True), tally.shape[1:])
             tally[6] = seen if r == ZERO else tally[6] + seen
             if r == ZERO:
                 norm_out[...] = norm
+        lse_cols[...] = jnp.transpose(jnp.broadcast_to(norms[0], (LANES, tokens)))
+        tag_cols[...] = jnp.transpose(jnp.broadcast_to(tags[0], (LANES, tokens)))
         arrive(swaps)
         for r in range(RING):
             zb[r, pl.ds(other, half), :] = theirs[r, ZERO:half].astype(BF16)
@@ -449,25 +437,17 @@
                 for c in range(TWO)]
         votes = FanSum(wires, 'y', lambda turn: tally.at[6], tally.at[pl.ds(0, 3)])
 
-        def unit(u, carry):
-            c, turn = lax.rem(u, TWO), lax.div(u, TWO)
-            ahead = lax.rem(2 + 3 * turn + 3 * lax.div(turn * (turn - ONE), TWO), RING)
-            p = c * RING + lax.rem(at['y'] + (at['z'] - at['y']) * c + ahead, RING)
-            first_row = at['x'] * SLICE + p * PIECE
-            whole = first_row + PIECE <= vocab
-
-            @pl.when(whole)
+        def unit(h, carry):
+            p, side, slot, first_row = fetch(h, end)
+
+            @pl.when(h + ONE < RING * RING)
             def _():
-                pltpu.make_async_copy(w_ref.at[pl.ds(ZERO, PIECE)], w_all.at[p], local.at[len(packets) + p]).wait()
-
-            @pl.when(jnp.logical_not(whole))
-            def _():
-                pltpu.make_async_copy(w_ref.at[pl.ds(ZERO, vocab % PIECE)], w_all.at[p, pl.ds(ZERO, vocab % PIECE)], local.at[len(packets) + p]).wait()
-
-            w, bias = w_all[p], bias_ref[p]
-            row = (iota((PIECE, LANES), ZERO) + first_row).astype(F32)
-
+                fetch(h + ONE, begin)
+
+            w, bias = w_bufs[slot], col_bufs[slot]
+            row = (iota((block, LANES), ZERO) + first_row).astype(F32)
             logits = dot(w, zb[0], NT)
+            out = []
             for r in range(RING):
                 zr, norm, tag, l = zb[r], norms[r], tags[r], logits
                 if r + ONE < RING:
@@ -476,92 +456,143 @@
                 for part in chunks(tokens):
                     prob = jnp.exp(l[:, part] + bias - norm[:, part])
                     grads.append((prob - jnp.where(row == tag[:, part], 1.0, 0.0)).astype(BF16))
-                out = dot(jnp.concatenate(grads, axis=ONE), zr, NN).reshape(RING, UNIT, dim)
-                acc[p] = acc[p] + out if r else out
+                out.append(dot(jnp.concatenate(grads, axis=ONE), zr, NN))
+            acc[p, pl.ds(side * TWO, TWO)] = sum(out).reshape(TWO, UNIT, dim)
+
             for c, total in enumerate(sums):
-                pl.when(u == c)(functools.partial(start, total.first))
-                pl.when(u == c + TWO)(functools.partial(start, total.plain[:1]))
-
-                @pl.when(u == c + RING)
-                def _(total=total):
-                    start(total.plain[1:])
-                    total.relay()
-
+                for s in range(TWO):
+                    here = TWO * c + s
+                    pl.when(h == here)(functools.partial(start, total.first[s:s + ONE]))
+                    pl.when(h == here + RING)(functools.partial(start, total.plain[s:s + ONE]))
+                    pl.when(h == here + TWO * RING)(functools.partial(total.relay, (s,)))
             return carry
 
         start(votes.lines)
-        lax.fori_loop(ZERO, TWO * RING, unit, ZERO)
-        tally[7] = votes.result()
-        votes = FanSum(wires, 'z', lambda turn: tally.at[7], tally.at[pl.ds(3, 3)])
-        start(votes.lines)
+        lax.fori_loop(ZERO, RING * RING, unit, ZERO)
+
+        last = (tiles - ONE) * tile
+
+        def fetch_tile(i, act):
+            slot = lax.rem(i, TWO)
+
+            def move(size):
+                act(pltpu.make_async_copy(w_ref.at[pl.ds(pl.multiple_of(i * tile, tile), size)], big_w.at[slot, pl.ds(ZERO, size)], local.at[slot]))
+
+            pl.when(i < tiles - ONE)(functools.partial(move, tile))
+            pl.when(i == tiles - ONE)(functools.partial(move, vocab - last))
+            return slot
 
         seconds = []
         for c, (axis, side) in enumerate(colors):
             kept = c * RING + at[axis]
-            acc[kept] = sums[c].result()
             seconds.append(RingSum(wires, side, functools.partial(lambda kept, side, turn: acc.at[kept, beside(side, turn)], kept, side),
                                    halves, [lanes[4].at[c], lanes[5].at[c]], [lanes[6].at[c], lanes[7].at[c]]))
-            start(seconds[c].first + seconds[c].plain)
-        for total in seconds:
-            total.relay()
-        for c, total in enumerate(seconds):
-            shard[c] = total.result()
-        count_out[...] = votes.result()
-
-        keep, steps = [], []
+        more_votes = FanSum(wires, 'z', lambda turn: tally.at[7], tally.at[pl.ds(3, 3)])
+        keep, steps, nexts = [], [], []
         for n, (rows, offset, c, order, way) in enumerate(PARTS):
             a1, a2, _ = ORDERS[order]
-            source = shard.at[c, pl.ds(offset, rows)]
             home = functools.partial(lambda n, a1, a2, turn: outs[n].at[at[a2], beside(a1, turn)], n, a1, a2)
-            keep.append(pltpu.make_async_copy(source, home(ZERO), local.at[len(packets) + TWO * RING + n]))
-            keep[n].start()
-            gather = RingGather(wires, a1, home, [(way, pl.ds(ZERO, rows))])
-            steps.append(gather)
-        for copy in keep:
-            copy.wait()
-        for gather in steps:
-            start(gather.step)
-        for gather in steps:
-            gather.forward()
-        nexts = []
-        for n, (rows, _, _, order, way) in enumerate(PARTS):
-            _, a2, _ = ORDERS[order]
-            steps[n].result()
+            keep.append(functools.partial(lambda n, c, offset, rows, home: pltpu.make_async_copy(
+                shard.at[c, pl.ds(offset, rows)], home(ZERO), local.at[RING + n_packets + n]), n, c, offset, rows, home))
+            steps.append(RingGather(wires, a1, home, [(way, pl.ds(ZERO, rows))]))
             nexts.append(RingGather(wires, a2, functools.partial(lambda n, a2, turn: outs[n].at[beside(a2, turn)], n, a2), [(way, pl.ds(ZERO, RING))]))
-            start(nexts[n].step)
-        for gather in nexts:
-            gather.forward()
+
+        def first_sums():
+            tally[7] = votes.result()
+            start(more_votes.lines)
+            for c, (axis, _) in enumerate(colors):
+                acc[c * RING + at[axis]] = sums[c].result()
+                start(seconds[c].first + seconds[c].plain)
+
+        def second_sums():
+            for c, total in enumerate(seconds):
+                shard[c] = total.result()
+            count_out[...] = more_votes.result()
+            for copy in keep:
+                copy().start()
+            for copy in keep:
+                copy().wait()
+            for gather in steps:
+                start(gather.step)
+
+        def second_axis():
+            for gather, onward in zip(steps, nexts):
+                gather.result()
+                start(onward.step)
+
+        def relays(group):
+            for one in group:
+                one.relay()
+
+        events = {2: first_sums, 4: lambda: relays(seconds), 7: second_sums, 9: lambda: relays(steps), 11: second_axis, 18: lambda: relays(nexts)}
+
+        def gz_tile(i, carry):
+            slot = fetch_tile(i, end)
+
+            @pl.when(i + ONE < tiles)
+            def _():
+                fetch_tile(i + ONE, begin)
+
+            w = big_w[slot]
+            l = dot(zb[0], w, NT) + bias_ref[i]
+            norm, rel = lse_cols[...], tag_cols[...] - (i * tile).astype(F32)
+            lane = iota((tokens, LANES), ONE).astype(F32)
+            grads, targets = [], []
+            for c in chunks(tile):
+                hit = lane == rel - c.start
+                grads.append(jnp.exp(l[:, c] - norm) - jnp.where(hit, 1.0, 0.0))
+                targets.append(jnp.where(hit, l[:, c], 0.0))
+            t_ref[...] += sum(targets)
+            grad = jnp.concatenate(grads, axis=ONE)
+            gb_ref[i] = jnp.sum(grad.reshape(-1, SUBLANES, tile), axis=ZERO)
+            gz_ref[...] += dot(grad.astype(BF16), w, NN)
+            for when, act in events.items():
+                pl.when(i + ONE == when)(act)
+            return carry
+
+        gz_ref[...] = jnp.zeros_like(gz_ref)
+        t_ref[...] = jnp.zeros_like(t_ref)
+        fetch_tile(ZERO, begin)
+        lax.fori_loop(ZERO, tiles, gz_tile, ZERO)
         for gather in nexts:
             gather.result()
         wires.finish()
 
-    copies = len(group) + len(packets) + TWO * 3 + TWO * TWO * 6 + len(PARTS) * TWO * 3
+    copies = len(group) + n_packets + TWO * 3 + TWO * TWO * 6 + n_parts * TWO * 3
     row_vector = pltpu.VMEM((RING, ONE, tokens), F32)
     packet = pltpu.VMEM((RING, *packets[0].shape), F32)
+    column = pltpu.VMEM((tokens, LANES), F32)
     lane = lambda *shape: [pltpu.VMEM((TWO, *shape, dim), F32)]
     return pl.pallas_call(
-        kernel, in_specs=[WHOLE] + [ANY] * len(packets) + [ANY, WHOLE], out_specs=[ANY] * len(PARTS) + [WHOLE] * TWO,
-        out_shape=[struct((RING, RING, part[0], dim)) for part in PARTS] + [struct((SUBLANES, LANES)), struct((ONE, tokens))],
-        scratch_shapes=[pltpu.VMEM((TWO * RING, RING, UNIT, dim), F32), pltpu.VMEM((TWO * RING, PIECE, dim), BF16),
+        kernel, in_specs=[WHOLE] + [ANY] * n_packets + [ANY, ANY, WHOLE], out_specs=[ANY] * n_parts + [WHOLE] * 5,
+        out_shape=[struct((RING, RING, part[0], dim)) for part in PARTS] + [struct((SUBLANES, LANES)), struct((ONE, tokens)),
+                   struct((tokens, dim)), struct((tokens, LANES)), struct((tiles, SUBLANES, tile))],
+        scratch_shapes=[pltpu.VMEM((TWO * RING, RING, UNIT, dim), F32), pltpu.VMEM((TWO, block, dim), BF16), pltpu.VMEM((TWO, block, LANES), F32),
                         pltpu.VMEM((RING, tokens, dim), BF16), packet, packet, pltpu.VMEM((TWO * RING, TWO, tokens), F32),
                         row_vector, row_vector, pltpu.VMEM((TWO, UNIT, dim), F32), pltpu.VMEM((TWO * RING, SUBLANES, LANES), F32),
+                        pltpu.VMEM((TWO, tile, dim), BF16), column, column,
                         *lane(TWO, UNIT) * TWO, *lane(RING, UNIT) * TWO, *lane(low), *lane(UNIT - low), *lane(UNIT) * TWO,
                         pltpu.SemaphoreType.DMA((copies,)), pltpu.SemaphoreType.DMA((copies,)),
-                        pltpu.SemaphoreType.DMA((len(packets) + TWO * RING + len(PARTS),))],
-        compiler_params=params(1), cost_estimate=cost(160), name='head_gw',
-    )(stats, *packets, w_t, bias_cols)
-
-
-def chip_sum(inputs):
+                        pltpu.SemaphoreType.DMA((RING + n_packets + n_parts,))],
+        compiler_params=params(1), cost_estimate=cost(150), name='head_grads',
+    )(stats, *packets, w_t, bias_cols, bias_row.reshape(tiles, ONE, tile))
+
+
+def chip_sum(inputs, small, count_tile):
     count = len(BLOCK)
     flat = [piece for group in inputs for piece in group]
-    dim = flat[0].shape[-1]
+    n_flat = len(flat)
+    dim = small.shape[-1]
+    few = small.shape[0] // RING
 
     def kernel(*refs):
-        ins, outs, refs = refs[:len(flat)], refs[len(flat):len(flat) + count], refs[len(flat) + count:]
-        acc, bufs, (send, recv, local) = refs[:count], [refs[count * n:count * (n + ONE)] for n in range(ONE, 7)], refs[-3:]
+        ins, (small_ref, tile_ref), refs = refs[:n_flat], refs[n_flat:n_flat + TWO], refs[n_flat + TWO:]
+        outs, small_out, refs = refs[:count], refs[count], refs[count + ONE:]
+        acc, bufs = refs[:count], [refs[count * n:count * (n + ONE)] for n in range(ONE, 7)]
+        over_x, over_y, over_z, sums, send, recv, local = refs[7 * count:]
         at, beside = coordinates()
         wires = Wires(send, recv)
+        scale = 1.0 / tile_ref[0:1, 0:1]
         entered = greet([((a, t),) for a in DP for t in range(ONE, RING)])
         loads, used = [[] for _ in BLOCK], ZERO
         for k, group in enumerate(inputs):
@@ -572,66 +603,78 @@
                 loads[k][-1].start()
                 row, used = row + rows, used + ONE
         entered()
+
+        def cell(ref, k, fixed, free):
+            axes = ORDERS[BLOCK[k]]
+            return lambda turn: ref[k].at[(*(at[a] for a in axes[:fixed]), *(beside(a, turn) for a in axes[fixed:free]))]
+
+        little = FanSum(wires, 'x', lambda turn: small_ref.at[beside('x', turn)], over_x)
+        start(little.lines)
         stages = []
-        for k, (_, order) in enumerate(BLOCK):
-            a1 = ORDERS[order][0]
-            stages.append(RingSum(wires, a1, functools.partial(lambda k, a1, turn: acc[k].at[beside(a1, turn)], k, a1),
-                                  HALVES, [bufs[0][k], bufs[1][k]], [bufs[2][k], bufs[3][k]]))
+        for k, order in enumerate(BLOCK):
+            stages.append(RingSum(wires, ORDERS[order][0], cell(acc, k, 0, 1), HALVES, [bufs[0][k], bufs[1][k]], [bufs[2][k], bufs[3][k]]))
             for load in loads[k]:
                 load.wait()
             start(stages[k].first + stages[k].plain)
+        sums[0] = little.result()
+        little = FanAll(wires, 'y', sums.at[0], over_y)
+        start(little.lines)
         for stage in stages:
             stage.relay()
-        for k, (_, order) in enumerate(BLOCK):
-            a1, a2, _ = ORDERS[order]
-            acc[k][at[a1]] = stages[k].result()
-            stages[k] = FanSum(wires, a2, functools.partial(lambda k, a1, a2, turn: acc[k].at[at[a1], beside(a2, turn)], k, a1, a2), bufs[4][k])
-            start(stages[k].lines)
-        for k, (_, order) in enumerate(BLOCK):
-            a1, a2, a3 = ORDERS[order]
-            acc[k][at[a1], at[a2]] = stages[k].result()
-            stages[k] = FanSum(wires, a3, functools.partial(lambda k, a1, a2, a3, turn: acc[k].at[at[a1], at[a2], beside(a3, turn)], k, a1, a2, a3), bufs[5][k])
-            start(stages[k].lines)
-        for k, (_, order) in enumerate(BLOCK):
-            a1, a2, a3 = ORDERS[order]
-            outs[k][at[a1], at[a2], at[a3]] = stages[k].result()
-            stages[k] = FanGather(wires, a3, functools.partial(lambda k, a1, a2, a3, turn: outs[k].at[at[a1], at[a2], beside(a3, turn)], k, a1, a2, a3))
+        sums[1] = little.result()
+        little = FanAll(wires, 'z', sums.at[1], over_z)
+        start(little.lines)
+        for level in (ONE, TWO):
+            for k, order in enumerate(BLOCK):
+                whole = cell(acc, k, level, level)(ZERO)
+                whole[...] = stages[k].result()
+                stages[k] = FanSum(wires, ORDERS[order][level], cell(acc, k, level, level + ONE), bufs[3 + level][k])
+                start(stages[k].lines)
+        small_out[at['x']] = little.result() * scale
+        little = FanGather(wires, 'x', lambda turn: small_out.at[beside('x', turn)])
+        start(little.step)
+        for k, order in enumerate(BLOCK):
+            whole = cell(outs, k, 3, 3)(ZERO)
+            whole[...] = stages[k].result() * scale
+            stages[k] = FanGather(wires, ORDERS[order][TWO], cell(outs, k, 2, 3))
             start(stages[k].step)
-        for k, (_, order) in enumerate(BLOCK):
-            a1, a2, _ = ORDERS[order]
+        for k, order in enumerate(BLOCK):
             stages[k].result()
-            stages[k] = FanGather(wires, a2, functools.partial(lambda k, a1, a2, turn: outs[k].at[at[a1], beside(a2, turn)], k, a1, a2))
+            stages[k] = FanGather(wires, ORDERS[order][ONE], cell(outs, k, 1, 2))
             start(stages[k].step)
-        for k, (_, order) in enumerate(BLOCK):
-            a1 = ORDERS[order][0]
+        for k, order in enumerate(BLOCK):
             stages[k].result()
-            stages[k] = RingGather(wires, a1, functools.partial(lambda k, a1, turn: outs[k].at[beside(a1, turn)], k, a1), list(enumerate(HALVES)))
+            stages[k] = RingGather(wires, ORDERS[order][0], cell(outs, k, 0, 1), list(enumerate(HALVES)))
             start(stages[k].step)
         for stage in stages:
-            stage.forward()
+            stage.relay()
         for stage in stages:
             stage.result()
+        little.result()
         wires.finish()
 
-    copies = count * (6 + 3 * RING + RING)
+    copies = count * (6 + 3 * RING + RING) + 3 * RING
 
     def buffers(*shape):
-        return [pltpu.VMEM((*shape, rows, dim), F32) for rows, _ in BLOCK]
-
+        return [pltpu.VMEM((*shape, ROWS, dim), F32)] * count
+
+    landing = pltpu.VMEM((RING, few, dim), F32)
     return pl.pallas_call(
-        kernel, in_specs=[ANY] * len(flat), out_specs=[WHOLE] * count,
-        out_shape=[struct((RING, RING, RING, rows, dim)) for rows, _ in BLOCK],
+        kernel, in_specs=[ANY] * n_flat + [WHOLE] * TWO, out_specs=[WHOLE] * (count + ONE),
+        out_shape=[struct((RING, RING, RING, ROWS, dim))] * count + [struct((RING, few, dim))],
         scratch_shapes=[*buffers(RING, RING, RING), *buffers(TWO, RING) * TWO, *buffers(RING, RING) * TWO, *buffers(3, RING), *buffers(3),
-                        pltpu.SemaphoreType.DMA((copies,)), pltpu.SemaphoreType.DMA((copies,)), pltpu.SemaphoreType.DMA((len(flat),))],
+                        pltpu.VMEM((3, few, dim), F32), landing, landing, pltpu.VMEM((TWO, few, dim), F32),
+                        pltpu.SemaphoreType.DMA((copies,)), pltpu.SemaphoreType.DMA((copies,)), pltpu.SemaphoreType.DMA((n_flat,))],
         compiler_params=params(2), cost_estimate=cost(60), name='chip_sum',
-    )(*flat)
+    )(*flat, small.reshape(RING, few, dim), count_tile)
 
 
 def place(groups, scale, coords, vocab, into=None):
     jobs = [(shift, n, array) for shift, arrays in groups for n, array in arrays.items()]
     dim = jobs[0][-1].shape[-1]
-    steps = RING * RING
+    steps = RING * TWO
     kept = () if into is None else (into,)
+    jobs_at = {(shift, n): j for j, (shift, n, _) in enumerate(jobs)}
 
     def kernel(coord_ref, scale_ref, *refs):
         ins, (out_ref, bufs, sems) = refs[:len(jobs)], refs[-3:]
@@ -639,17 +682,18 @@
 
         def each(step, act):
             slot = lax.rem(step, TWO)
-            for j, (shift, n, _) in enumerate(jobs):
+            for m, (shift, n, _) in itertools.product(range(TWO), jobs):
+                j = jobs_at[shift, n]
                 rows, offset, c, order, _ = PARTS[n]
                 a1, a2, a3 = ORDERS[order]
-                at = {a1: lax.rem(step, RING), a2: lax.div(step, RING), a3: lax.rem(coord_ref[DP.index(a3)] + shift, RING)}
+                at = {a1: lax.rem(step, TWO) * TWO + m, a2: lax.div(step, TWO), a3: lax.rem(coord_ref[DP.index(a3)] + shift, RING)}
                 first, second = (('y', 'z'), ('z', 'y'))[c]
                 row = pl.multiple_of(at['x'] * SLICE + c * HALF_SLICE + at[first] * PIECE + at[second] * UNIT + offset, SUBLANES)
                 edge = vocab % UNIT - offset
                 whole = row + rows <= vocab
 
                 def move(size):
-                    act(pltpu.make_async_copy(bufs.at[slot, j, pl.ds(ZERO, size)], out_ref.at[pl.ds(row, size)], sems.at[slot, j]))
+                    act(pltpu.make_async_copy(bufs.at[slot, j, m, pl.ds(ZERO, size)], out_ref.at[pl.ds(row, size)], sems.at[slot, m, j]))
 
                 pl.when(whole)(functools.partial(move, rows))
                 if ZERO < edge < rows:
@@ -660,7 +704,7 @@
             each(step - TWO, lambda copy: copy.wait())
 
         for j, (_, n, _) in enumerate(jobs):
-            bufs[lax.rem(step, TWO), j, ZERO:PARTS[n][0]] = ins[j][ZERO, ZERO] * scale_ref[ZERO]
+            bufs[lax.rem(step, TWO), j, :, ZERO:PARTS[n][0]] = ins[j][ZERO] * scale_ref[ZERO]
         each(step, lambda copy: copy.start())
 
         @pl.when(step == steps - ONE)
@@ -668,20 +712,35 @@
             each(step - ONE, lambda copy: copy.wait())
             each(step, lambda copy: copy.wait())
 
-    blocks = [pl.BlockSpec((ONE, ONE, PARTS[n][0], dim), lambda i: (i // RING, i % RING, ZERO, ZERO)) for _, n, _ in jobs]
+    blocks = [pl.BlockSpec((ONE, TWO, PARTS[n][0], dim), lambda i: (i // TWO, i % TWO, ZERO, ZERO)) for _, n, _ in jobs]
     return pl.pallas_call(
         kernel, grid=(steps,), in_specs=[SCALARS, SCALARS, *blocks] + [ANY for _ in kept], out_specs=ANY,
         out_shape=struct((vocab, dim)), input_output_aliases={TWO + len(jobs): ZERO for _ in kept},
-        scratch_shapes=[pltpu.VMEM((TWO, len(jobs), 72, dim), F32), pltpu.SemaphoreType.DMA((TWO, len(jobs)))],
+        scratch_shapes=[pltpu.VMEM((TWO, len(jobs), TWO, 72, dim), F32), pltpu.SemaphoreType.DMA((TWO, TWO, len(jobs)))],
         compiler_params=params(), cost_estimate=cost(2 * len(jobs)),
     )(coords, scale, *[array for *_, array in jobs], *kept)
 
 
-def norm_stats(values):
-    row_mean = jnp.mean(values, axis=-ONE, keepdims=True)
-    centered = values - row_mean
-    inv_std = lax.rsqrt(jnp.mean(centered * centered, axis=-ONE, keepdims=True) + LN_EPS)
-    return centered * inv_std, inv_std
+def norm_forward(terms, row, gain, shift):
+    tokens, dim = terms[0].shape
+
+    def kernel(row_ref, gain_ref, shift_ref, *refs):
+        ins, (bf_ref, out_ref, hat_ref, inv_ref) = refs[:len(terms)], refs[len(terms):]
+        first, *others = (ref[...].astype(F32) for ref in ins)
+        values = first + sum(others[1:], others[0]) + row_ref[...] if others else first
+        centered = values - jnp.mean(values, axis=-ONE, keepdims=True)
+        inv = lax.rsqrt(jnp.mean(centered * centered, axis=-ONE, keepdims=True) + LN_EPS)
+        hat = centered * inv
+        out = hat * gain_ref[...] + shift_ref[...]
+        bf_ref[...] = out.astype(BF16)
+        out_ref[...] = out
+        hat_ref[...] = hat
+        inv_ref[...] = inv
+
+    return pl.pallas_call(
+        kernel, out_shape=[struct((tokens, dim), BF16), struct((tokens, dim)), struct((tokens, dim)), struct((tokens, ONE))],
+        compiler_params=params(), cost_estimate=cost(2),
+    )(*(v[np.newaxis] for v in (row, gain, shift)), *terms)
 
 
 def norm_backward(grad_out, x_hat, inv_std, gain_vec):
@@ -725,18 +784,14 @@
         tables = rope_tables(tokens, head_dim)
         mask_f = loss_mask.astype(F32)
 
-        resid_in = hidden[ZERO].astype(F32)
-        ln_hat, ln_inv = norm_stats(resid_in)
-        normed = (ln_hat * ln_gain + ln_bias).astype(BF16)
+        normed, _, ln_hat, ln_inv = norm_forward([hidden[ZERO]], ln_bias, ln_gain, ln_bias)
         qs, k_rot, v_proj, context, lse_att = attn_fwd(normed, wq, wk, wv, *tables, score_scale)
         pre_act = dot(normed, w_fc_in, NN) + b_fc_in
         gelu_out, gelu_vjp = jax.vjp(functools.partial(jax.nn.gelu, approximate=True), pre_act)
         gelu_bf = gelu_out.astype(BF16)
         block_part = dot(context, wo, NN) + dot(gelu_bf, w_fc_out, NN)
-        resid_out = resid_in + (block_part + swap(block_part)) + b_fc_out
-        fin_hat, fin_inv = norm_stats(resid_out)
-        final_f32 = fin_hat * lnf_gain + lnf_bias
-        final_bf = final_f32.astype(BF16)
+        peer_part = hop(block_part, 'tp', SWAP)
+        final_bf, final_f32, fin_hat, fin_inv = norm_forward([hidden[ZERO], block_part, peer_part], b_fc_out, lnf_gain, lnf_bias)
 
         extra = jnp.concatenate([labels.astype(F32).reshape(TWO, half), mask_f.reshape(TWO, half), jnp.zeros((RING, half), F32)])
         packet = jnp.concatenate([lax.dynamic_slice_in_dim(final_f32, tp * half, half, ZERO), extra])
@@ -748,10 +803,10 @@
         bias_row = b_head[np.newaxis]
         bias_pad = jnp.concatenate([b_head, jnp.full((RING * SLICE - vocab,), NEG, F32)])
         bias_mine = lax.dynamic_slice_in_dim(bias_pad, lax.axis_index('x') * SLICE, SLICE, ZERO)
-        bias_cols = jnp.broadcast_to(bias_mine[:, np.newaxis], (SLICE, LANES)).reshape(-1, PIECE, LANES)
+        bias_cols = jnp.broadcast_to(bias_mine[:, np.newaxis], (SLICE, LANES)).reshape(-1, PIECE // TWO, LANES)
         partial = head_lse(final_bf, w_t, bias_row)
         stats = head_lse(final_bf, w_t, bias_row, partial)
-        *gathered, count, log_norm = head_gw(stats, [packet, *from_sides, *across], w_t, bias_cols)
+        *gathered, count, log_norm, grad_final, target, grad_b_head = head_grads(stats, [packet, *from_sides, *across], w_t, bias_cols, bias_pad[np.newaxis])
         scale = 1.0 / count[0, :1]
 
         last = [ORDERS[order][-1] for *_, order, _ in PARTS]
@@ -760,13 +815,6 @@
         from_right = [hop(g, a, LEFT) for g, a in zip(gathered, last)]
         far = [hop((from_left, from_right)[way][n], a, (RIGHT, LEFT)[way]) for n, (way, a) in enumerate(zip(ways, last))]
 
-        final_bf, _ = lax.optimization_barrier((final_bf, count))
-        own_mask = mask_f[0][:, np.newaxis] > ZERO
-        own_tag = labels[0][:, np.newaxis] - tp * vocab
-        wide = lambda column: jnp.broadcast_to(column, (tokens, LANES))
-        lse_b = wide(jnp.where(own_mask, log_norm.reshape(tokens, ONE), -NEG))
-        tag_b = wide(jnp.where(own_mask & (own_tag < vocab), own_tag, -ONE))
-        grad_final, target, grad_b_head = head_gz(final_bf, w_t, bias_row, lse_b, tag_b)
         hits = jnp.sum(target).reshape(ONE, ONE)
         loss_part = jnp.sum(mask_f * log_norm) - (hits + swap(hits))
         grad_final = grad_final + swap(grad_final)
@@ -782,28 +830,31 @@
         grad_normed = dot(grad_q, wq, NN) + dot(grad_k, wk, NN) + dot(grad_v, wv, NN) + dot(grad_pre, w_fc_in, NT)
         grad_normed = grad_normed + swap(grad_normed)
         grad_ln_in, grad_ln_gain, grad_ln_bias = norm_backward(grad_normed, ln_hat, ln_inv, ln_gain)
-        grad_hidden = ((grad_resid + grad_ln_in) * scale).astype(BF16)
+        grad_hidden = ((grad_resid + grad_ln_in) * scale).astype(BF16)[np.newaxis]
 
         vectors = [grad_ln_gain, grad_ln_bias, grad_b_fc_in, grad_b_fc_out, grad_lnf_gain, grad_lnf_bias,
-                   jnp.broadcast_to(loss_part[0], (dim,)), jnp.sum(grad_b_head, axis=ZERO)]
+                   jnp.broadcast_to(loss_part[0], (dim,)), jnp.sum(grad_b_head, axis=ONE).reshape(-1)]
         ends = list(np.cumsum([v.shape[0] for v in vectors]))
-        vectors.append(jnp.zeros((BLOCK[1][0] * RING ** 3 * dim - int(ends[-1]),), F32))
-        cube = lambda value, n: value.reshape(-1, RING, RING, BLOCK[n][0], dim)
-        first = [cube(dot(g, h, TN), 0) for g, h in ((grad_q, normed), (grad_k, normed), (grad_v, normed), (context, grad_block))]
-        sums = chip_sum((first, [cube(jnp.concatenate(vectors), 1)], [cube(dot(gelu_bf, grad_block, TN), 2)],
-                         [cube(dot(normed, grad_pre[:, cols], TN), 3) for cols in chunks(grad_pre.shape[-1], dim)]))
-        weights, small, fc_out, fc_in = (s.reshape(-1, dim) * scale for s in sums)
+        vectors.append(jnp.zeros((RING * FEW * dim - int(ends[-1]),), F32))
+        rows = jnp.concatenate([v.reshape(-1, dim) for v in vectors])
+        cube = lambda value: value.reshape(-1, RING, RING, ROWS, dim)
+        heads_grads = [cube(dot(g, h, TN)) for g, h in ((grad_q, normed), (grad_k, normed), (grad_v, normed), (context, grad_block))]
+        halves = chunks(grad_pre.shape[-1], dim)
+        outer = [[cube(dot(gelu_bf[:, cols], grad_block, TN))] for cols in halves]
+        inner = [[cube(dot(normed, grad_pre[:, cols], TN))] for cols in halves]
+        *sums, small = chip_sum([heads_grads[:TWO], outer[0], inner[0], heads_grads[TWO:], outer[1], inner[1]], rows, count)
+        sums = [s.reshape(-1, dim) for s in sums]
         pieces = [small.reshape(-1)[end - v.shape[0]:end] for v, end in zip(vectors, ends)]
-        back = lambda n: jnp.moveaxis(weights[n * lanes:(n + ONE) * lanes].reshape(heads, head_dim, dim), -ONE, ZERO)
+        weights = [sums[n // TWO * 3][n % TWO * lanes:(n % TWO + ONE) * lanes].reshape(heads, head_dim, dim) for n in range(RING)]
+        weights[:3] = [jnp.moveaxis(w, -ONE, ZERO) for w in weights[:3]]
+        loss, grad_b_head = pieces[6][0], pieces[7][:vocab]
+        fc_in, fc_out = jnp.concatenate([sums[2], sums[5]], axis=ONE), jnp.concatenate([sums[1], sums[4]])
 
         coords = jnp.stack([lax.axis_index(a) for a in DP]).astype(jnp.int32)
         grad_w_head = place([(0, dict(enumerate(gathered)))], scale, coords, vocab)
         grad_w_head = place([(3, dict(enumerate(from_left))), (1, dict(enumerate(from_right)))], scale, coords, vocab, grad_w_head)
         grad_w_head = place([(2, dict(enumerate(far)))], scale, coords, vocab, grad_w_head)
-        gains = pieces[:2], pieces[2], pieces[3:6]
-        return (pieces[6][0], grad_hidden[np.newaxis], *gains[0], back(0), back(1), back(2),
-                weights[3 * lanes:].reshape(heads, head_dim, dim), jnp.concatenate([fc_in[:dim], fc_in[dim:]], axis=ONE),
-                gains[1], fc_out, *gains[2], grad_w_head.T, pieces[7][:vocab])
+        return (loss, grad_hidden, *pieces[:2], *weights, fc_in, pieces[2], fc_out, *pieces[3:6], grad_w_head.T, grad_b_head)
 
     return jax.shard_map(local_step, mesh=mesh, in_specs=DATA_SPECS + PARAM_SPECS,
                          out_specs=(P(), P(DP, None, None)) + PARAM_SPECS, check_vma=False)

time: 744 us -> 625 us (0.84)
  Pallas kernels: 481 us -> 407 us
  waiting for transfers between devices: 125 us -> 99.6 us
  other arithmetic: 30.9 us -> 19.3 us
    pallas_call x3 -> x4, Pallas kernels: 358 us -> 296 us  [the longest x1 169 us: head_grads(): pl.pallas_call(kernel, in_specs=[WHOLE] + [ANY] * n_packets + [ANY, ANY,...]
    ppermute x22 -> x23, waiting for transfers between devices: 122 us -> 99.6 us  [hop(): return lax.ppermute(value, axis, way)]
    pallas_call x3, Pallas kernels: 55 us -> 43.2 us  [place(): pl.pallas_call(kernel, grid=(steps,), in_specs=[SCALARS, SCALARS, *blocks...]
    dot_general x4 -> x0, local copies, waits for them, and re-layouts: 7.55 us -> none  [dot(): return lax.dot_general(a, b, dims, preferred_element_type=F32)]
    reduce_sum x5 -> x1, other arithmetic: 7.67 us -> 0.2 us  [local_step(): jnp.sum(grad_b_head, axis=ONE).reshape(-1)]
    ppermute x22 -> x23, starting transfers between devices: 31.4 us -> 28.9 us  [hop(): return lax.ppermute(value, axis, way)]
    dot_general x16 -> x17, matrix products: 35.6 us -> 37.8 us  [dot(): return lax.dot_general(a, b, dims, preferred_element_type=F32)]
  transfers between devices with their start and end apart: 26 -> 26, of which waited for: 7 -> 9; matrix products, arithmetic and copies ran while one was open for 9% -> 10% of each run, Pallas kernels for 29% -> 33%
where the time goes in v2:
time: 625 us; the launch traced here: 616 us
  Pallas kernels  407 us (65%)
  waiting for transfers between devices  99.6 us (16%)
  matrix products  37.8 us (6%)
  starting transfers between devices  28.9 us (5%)
  local copies, waits for them, and re-layouts  19.4 us (3%)
  other arithmetic  19.3 us (3%)
    pallas_call x1, Pallas kernels, head_grads(): pl.pallas_call(kernel, in_specs=[WHOLE] + [ANY] * n_packets + [ANY, ANY,...  169 us
    pallas_call x1, Pallas kernels, chip_sum(): pl.pallas_call(kernel, in_specs=[ANY] * n_flat + [WHOLE] * TWO, out_specs...  116 us
    ppermute x23, waiting for transfers between devices, hop(): return lax.ppermute(value, axis, way)  99.6 us
    pallas_call x3, Pallas kernels, place(): pl.pallas_call(kernel, grid=(steps,), in_specs=[SCALARS, SCALARS, *blocks...  43.2 us
    pallas_call x2, Pallas kernels, head_lse(): pl.pallas_call(kernel, grid=(early if first else steps - early,), in_spec...  42 us
    dot_general x17, matrix products, dot(): return lax.dot_general(a, b, dims, preferred_element_type=F32)  37.8 us
    ppermute x23, starting transfers between devices, hop(): return lax.ppermute(value, axis, way)  28.9 us
    pallas_call x1, Pallas kernels, attn_bwd(): pl.pallas_call(kernel, grid=(lanes // LANES,), in_specs=[pair] * RING + [...  13 us
  transfers between devices with their start and end apart: 26, of which 9 were waited for; matrix products, arithmetic and copies ran while one was open for 10% of the time, Pallas kernels for 33%

profile of v2, /device:TPU:0, one launch (start us, length us, event | category | flops | bytes accessed | tf_op | source)
XLA Modules:
  0.0 616.4 jit_solution(899933963112044604)
XLA Ops:
  0.7 4.7 shard_map.306
  5.4 5.3 multiply_convert_fusion
  10.7 2.6 fusion.20
  13.3 12.9 %attn_fwd.1 = (bf16[1024,256]{1,0:T(8,128)(2,1)}, bf16[1024,256]{1,0:T(8,128)(2,1)}, bf16[1024,256]{1,0:T(8,128)(2,1)}, bf16[1024,256]{1,0:T(8,128)(2,1)}, f32[2,2,1024]{2,1,0:T(2,128)}) custom-call(bf16[1024,512]{1,0:T(8,128)(2,1)} %get-tuple-element.51.u_ref, bf16[256,512]{1,0:T(8,128)(2,1)} %bitcast.113, bf16[256,512]{1,0:T(8,128)(2,1)} %bitcast.111, ...), custom_call_target="tpu_custom_call" | custom-call | flops 12999999488 | bytes 1 | tf_op jit(solution)/shard_map/attn_fwd/pallas_call | solution.py:175
  32.9 6.0 shard_map.307
  40.4 2.9 collective-permute-start.2
  43.5 24.0 %head_lse_first.1 = (f32[1024,128]{1,0:T(8,128)}, f32[1024,128]{1,0:T(8,128)}) custom-call(bf16[1024,512]{1,0:T(8,128)(2,1)} %get-tuple-element.57.z_ref, bf16[25152,512]{1,0:T(8,128)(2,1)} %bitcast.125, f32[1,25152]{1,0:T(1,128)} %broadcast_in_dim.52.b_ref), custom_call_target="tpu_custom_call" | custom-call | flops 19000000512 | bytes 1 | tf_op jit(solution)/shard_map/head_lse_first/pallas_call | solution.py:126
  67.6 3.3 collective-permute-start.4
  72.0 18.0 %head_lse_rest.1.stats_ref = f32[2,1024]{1,0:T(2,128)} custom-call(bf16[1024,512]{1,0:T(8,128)(2,1)} %get-tuple-element.57.z_ref, bf16[25152,512]{1,0:T(8,128)(2,1)} %bitcast.126, f32[1,25152]{1,0:T(1,128)} %broadcast_in_dim.52.b_ref, f32[1024,128]{1,0:T(8,128)} %get-tuple-element.58.refs_0_, f32[1024,128]{1,0:T(8,128)} %get-tuple-element.59.refs_1_), custom_call_target="tpu_custom_call" | custom-call | flops 19000000512 | bytes 1 | tf_op jit(solution)/shard_map/head_lse_rest/pallas_call | solution.py:126
  92.2 168.7 %head_grads.1 = (f32[4,4,72,512]{3,2,1,0:T(8,128)}, f32[4,4,64,512]{3,2,1,0:T(8,128)}, f32[4,4,64,512]{3,2,1,0:T(8,128)}, f32[4,4,64,512]{3,2,1,0:T(8,128)}, f32...) custom-call(f32[2,1024]{1,0:T(2,128)} %head_lse_rest.1.stats_ref, ...), custom_call_target="tpu_custom_call" | custom-call | flops 149999992832 | bytes 1 | tf_op jit(solution)/shard_map/head_grads/pallas_call | solution.py:566
  266.0 3.2 collective-permute-start.14
  272.5 12.1 %shard_map.308.refs_12_ = f32[25152,512]{1,0:T(8,128)} custom-call(s32[3]{0:T(128)} %pad_add_fusion.coord_ref, f32[1]{0:T(128)} %bitcast.52.scale_ref, f32[4,4,72,512]{3,2,1,0:T(8,128)} %get-tuple-element.80.refs_0_, f32[4,4,64,512]{3,2,1,0:T(8,128)} %get-tuple-element.81.refs_1_, f32[4,4,64,512]{3,2,1,0:T(8,128)} %get-tuple-element.82.refs_2_, ...), custom_call_target="tpu_custom_call" | custom-call | flops 12000000000 | bytes 1 | tf_op jit(solution)/shard_map/pallas_call | solution.py:716
  286.8 3.2 multiply_reduce_fusion.1
  292.9 13.0 %attn_bwd.1 = (bf16[1024,256]{1,0:T(8,128)(2,1)}, bf16[1024,256]{1,0:T(8,128)(2,1)}, bf16[1024,256]{1,0:T(8,128)(2,1)}) custom-call(bf16[1024,256]{1,0:T(8,128)(2,1)} %get-tuple-element.52.qs_ref, bf16[1024,256]{1,0:T(8,128)(2,1)} %get-tuple-element.53.k_ref, bf16[1024,256]{1,0:T(8,128)(2,1)} %get-tuple-element.54.v_ref, ...), custom_call_target="tpu_custom_call" | custom-call | flops 12999999488 | bytes 1 | tf_op jit(solution)/shard_map/attn_bwd/pallas_call | solution.py:216
  305.9 6.3 %collective-permute-done.10.refs_7_ = f32[4,4,64,512]{3,2,1,0:T(8,128)} collective-permute-done((f32[4,4,64,512]{3,2,1,0:T(8,128)}, f32[4,4,64,512]{3,2,1,0:T(8,128)}, u32[]{:S(2)}, u32[]{:S(2)}) %collective-permute-start.10) | collective-permute-done | bytes 2097184 | tf_op jit(solution)/shard_map/ppermute | solution.py:765
  312.3 2.5 fusion.24
  315.2 2.7 collective-permute-start.24
  322.9 5.0 fusion.16
  329.2 5.0 collective-permute-done.16.refs_4_
  336.3 24.5 %collective-permute-done.21.refs_3_ = f32[4,4,64,512]{3,2,1,0:T(8,128)S(1)} collective-permute-done((f32[4,4,64,512]{3,2,1,0:T(8,128)}, f32[4,4,64,512]{3,2,1,0:T(8,128)S(1)}, u32[]{:S(2)}, u32[]{:S(2)}) %collective-permute-start.21) | collective-permute-done | bytes 2097184 | tf_op jit(solution)/shard_map/ppermute | solution.py:765
  366.1 3.4 fusion.9
  379.4 45.9 %collective-permute-done.25.refs_10_ = f32[4,4,64,512]{3,2,1,0:T(8,128)} collective-permute-done((f32[4,4,64,512]{3,2,1,0:T(8,128)}, f32[4,4,64,512]{3,2,1,0:T(8,128)}, u32[]{:S(2)}, u32[]{:S(2)}) %collective-permute-start.25) | collective-permute-done | bytes 2097184 | tf_op jit(solution)/shard_map/ppermute | solution.py:765
  425.3 3.3 collective-permute-start.11
  428.6 3.2 collective-permute-start.15
  431.8 19.3 %shard_map.309.refs_6_ = f32[25152,512]{1,0:T(8,128)} custom-call(s32[3]{0:T(128)} %pad_add_fusion.coord_ref, f32[1]{0:T(128)} %bitcast.52.scale_ref, f32[4,4,72,512]{3,2,1,0:T(8,128)} %collective-permute-done.8.refs_0_, f32[4,4,64,512]{3,2,1,0:T(8,128)} %collective-permute-done.20.refs_1_, ...), custom_call_target="tpu_custom_call", output_to_operand_aliasing={{}: (14, {})} | custom-call | flops 24000000000 | bytes 1 | tf_op jit(solution)/shard_map/pallas_call | solution.py:716
  451.1 3.3 collective-permute-start.19
  454.5 4.8 multiply_reduce_fusion
  459.3 2.6 concatenate.17
  461.9 12.6 %collective-permute-done.11.refs_1_ = f32[4,4,64,512]{3,2,1,0:T(8,128)} collective-permute-done((f32[4,4,64,512]{3,2,1,0:T(8,128)}, f32[4,4,64,512]{3,2,1,0:T(8,128)}, u32[]{:S(2)}, u32[]{:S(2)}) %collective-permute-start.11) | collective-permute-done | bytes 2097184 | tf_op jit(solution)/shard_map/ppermute | solution.py:765
  474.8 116.5 %chip_sum.1 = (f32[4,4,4,8,512]{4,3,2,1,0:T(8,128)}, f32[4,4,4,8,512]{4,3,2,1,0:T(8,128)}, f32[4,4,4,8,512]{4,3,2,1,0:T(8,128)}, f32[4,4,4,8,512]{4,3,2,1,0:T(8,...) custom-call(f32[2,4,4,8,512]{4,3,2,1,0:T(8,128)} %bitcast.99, ...), custom_call_target="tpu_custom_call" | custom-call | flops 60000002048 | bytes 1 | tf_op jit(solution)/shard_map/chip_sum/pallas_call | solution.py:662
  593.9 3.2 pad_maximum_fusion.1
  604.0 11.9 %shard_map.310 = f32[25152,512]{1,0:T(8,128)} custom-call(s32[3]{0:T(128)} %pad_add_fusion.coord_ref, f32[1]{0:T(128)} %bitcast.52.scale_ref, f32[4,4,72,512]{3,2,1,0:T(8,128)} %collective-permute-done.9.refs_0_, f32[4,4,64,512]{3,2,1,0:T(8,128)} %collective-permute-done.11.refs_1_, ...), custom_call_target="tpu_custom_call", output_to_operand_aliasing={{}: (8, {})} | custom-call | flops 12000000000 | bytes 1 | tf_op jit(solution)/shard_map/pallas_call | solution.py:716
  (194 shorter events, 56.2 us)
Async XLA Ops:
  28.5 4.4 collective-permute-start
  40.3 27.2 %copy-start.20 = (f32[520,512]{1,0:T(8,128)}, f32[520,512]{1,0:T(8,128)S(1)}, u32[]{:S(2)}) copy-start(f32[520,512]{1,0:T(8,128)S(1)} %maximum_maximum_fusion.refs_0_) | copy-start | bytes 3194884
  40.4 27.1 %collective-permute-start.2 = (f32[520,512]{1,0:T(8,128)S(1)}, f32[520,512]{1,0:T(8,128)S(1)}, u32[]{:S(2)}, u32[]{:S(2)}) collective-permute-start(f32[520,512]{1,0:T(8,128)S(1)} %maximum_maximum_fusion.refs_0_), channel_id=1, source_target_pairs={{0,3},{1,0},{2,1},{3,2},{4,7},{5,4},{6,5},{7,6},{8,11},{9,8},{10,9... | collective-permute-start | bytes 3194888 | tf_op jit(solution)/shard_map/ppermute | solution.py:765
  43.3 27.5 %collective-permute-start.1 = (f32[520,512]{1,0:T(8,128)S(1)}, f32[520,512]{1,0:T(8,128)}, u32[]{:S(2)}, u32[]{:S(2)}) collective-permute-start(f32[520,512]{1,0:T(8,128)S(1)} %maximum_maximum_fusion.refs_0_), channel_id=1, source_target_pairs={{0,1},{1,2},{2,3},{3,0},{4,5},{5,6},{6,7},{7,4},{8,9},{9,10},{10,1... | collective-permute-start | bytes 3194888 | tf_op jit(solution)/shard_map/ppermute | solution.py:765
  67.5 22.5 %copy-start.31 = (f32[520,512]{1,0:T(8,128)}, f32[520,512]{1,0:T(8,128)S(1)}, u32[]{:S(2)}) copy-start(f32[520,512]{1,0:T(8,128)S(1)} %collective-permute-done.2.refs_2_) | copy-start | bytes 3194884
  67.6 22.5 %collective-permute-start.4 = (f32[264,512]{1,0:T(8,128)S(1)}, f32[264,512]{1,0:T(8,128)}, u32[]{:S(2)}, u32[]{:S(2)}) collective-permute-start(f32[264,512]{1,0:T(8,128)S(1)} %slice.85), channel_id=1, source_target_pairs={{0,3},{1,0},{2,1},{3,2},{4,7},{5,4},{6,5},{7,6},{8,11},{9,8},{10,9... | collective-permute-start | bytes 1622024 | tf_op jit(solution)/shard_map/ppermute | solution.py:765
  71.9 18.1 %collective-permute-start.3 = (f32[256,512]{1,0:T(8,128)S(1)}, f32[256,512]{1,0:T(8,128)S(1)}, u32[]{:S(2)}, u32[]{:S(2)}) collective-permute-start(f32[256,512]{1,0:T(8,128)S(1)} %slice.84), channel_id=1, source_target_pairs={{0,1},{1,2},{2,3},{3,0},{4,5},{5,6},{6,7},{7,4},{8,9},{9,10},{10,1... | collective-permute-start | bytes 1572872 | tf_op jit(solution)/shard_map/ppermute | solution.py:765
  92.2 168.8 %copy-start.29 = (f32[1024,1]{1,0:T(8,128)S(1)}, f32[1024,1]{1,0:T(8,128)}, u32[]{:S(2)}) copy-start(f32[1024,1]{1,0:T(8,128)} %get-tuple-element.73) | copy-start | bytes 12292
  92.2 170.2 %copy-start.30 = (f32[1024,1]{1,0:T(8,128)S(1)}, f32[1024,1]{1,0:T(8,128)}, u32[]{:S(2)}) copy-start(f32[1024,1]{1,0:T(8,128)} %get-tuple-element.56) | copy-start | bytes 12292
  261.0 25.7 %collective-permute-start.5 = (f32[1024,512]{1,0:T(8,128)}, f32[1024,512]{1,0:T(8,128)}, u32[]{:S(2)}, u32[]{:S(2)}) collective-permute-start(f32[1024,512]{1,0:T(8,128)} %get-tuple-element.61), channel_id=1, source_target_pairs={{0,64},{64,0},{1,65},{65,1},{2,66},{66,2},{3,67},{67,3},{4,68},{68... | collective-permute-start | bytes 6291464 | tf_op jit(solution)/shard_map/ppermute | solution.py:779
  263.9 48.3 %collective-permute-start.10 = (f32[4,4,64,512]{3,2,1,0:T(8,128)}, f32[4,4,64,512]{3,2,1,0:T(8,128)}, u32[]{:S(2)}, u32[]{:S(2)}) collective-permute-start(f32[4,4,64,512]{3,2,1,0:T(8,128)} %get-tuple-element.81.refs_1_), channel_id=1, source_target_pairs={{0,48},{16,0},{32,16},{48,32},{1,49},{17,1},{33,17},{49,33},{2,50}... | collective-permute-start | bytes 6291464 | tf_op jit(solution)/shard_map/ppermute | solution.py:765
  266.0 49.3 %collective-permute-start.12 = (f32[4,4,64,512]{3,2,1,0:T(8,128)}, f32[4,4,64,512]{3,2,1,0:T(8,128)}, u32[]{:S(2)}, u32[]{:S(2)}) collective-permute-start(f32[4,4,64,512]{3,2,1,0:T(8,128)} %get-tuple-element.82.refs_2_), channel_id=1, source_target_pairs={{0,1},{1,2},{2,3},{3,0},{4,5},{5,6},{6,7},{7,4},{8,9},{9,10},{10,1... | collective-permute-start | bytes 6291464 | tf_op jit(solution)/shard_map/ppermute | solution.py:765
  266.0 61.9 %collective-permute-start.14 = (f32[4,4,64,512]{3,2,1,0:T(8,128)}, f32[4,4,64,512]{3,2,1,0:T(8,128)}, u32[]{:S(2)}, u32[]{:S(2)}) collective-permute-start(f32[4,4,64,512]{3,2,1,0:T(8,128)} %get-tuple-element.83.refs_3_), channel_id=1, source_target_pairs={{0,3},{1,0},{2,1},{3,2},{4,7},{5,4},{6,5},{7,6},{8,11},{9,8},{10,9... | collective-permute-start | bytes 6291464 | tf_op jit(solution)/shard_map/ppermute | solution.py:765
  271.0 13.7 %collective-permute-start.7 = (f32[1,1]{1,0:T(1,128)}, f32[1,1]{1,0:T(1,128)}, u32[]{:S(2)}, u32[]{:S(2)}) collective-permute-start(f32[1,1]{1,0:T(1,128)} %bitcast.32), channel_id=1, source_target_pairs={{0,64},{64,0},{1,65},{65,1},{2,66},{66,2},{3,67},{67,3},{4,68},{68... | collective-permute-start | bytes 20 | tf_op jit(solution)/shard_map/ppermute | solution.py:779
  284.6 49.6 %collective-permute-start.16 = (f32[4,4,64,512]{3,2,1,0:T(8,128)}, f32[4,4,64,512]{3,2,1,0:T(8,128)}, u32[]{:S(2)}, u32[]{:S(2)}) collective-permute-start(f32[4,4,64,512]{3,2,1,0:T(8,128)} %get-tuple-element.84.refs_4_), channel_id=1, source_target_pairs={{0,4},{4,8},{8,12},{12,0},{1,5},{5,9},{9,13},{13,1},{2,6},{6,10},{... | collective-permute-start | bytes 6291464 | tf_op jit(solution)/shard_map/ppermute | solution.py:765
  286.7 49.6 %collective-permute-start.20 = (f32[4,4,64,512]{3,2,1,0:T(8,128)}, f32[4,4,64,512]{3,2,1,0:T(8,128)}, u32[]{:S(2)}, u32[]{:S(2)}) collective-permute-start(f32[4,4,64,512]{3,2,1,0:T(8,128)} %get-tuple-element.81.refs_1_), channel_id=1, source_target_pairs={{0,16},{16,32},{32,48},{48,0},{1,17},{17,33},{33,49},{49,1},{2,18}... | collective-permute-start | bytes 6291464 | tf_op jit(solution)/shard_map/ppermute | solution.py:765
  312.2 48.6 %collective-permute-start.21 = (f32[4,4,64,512]{3,2,1,0:T(8,128)}, f32[4,4,64,512]{3,2,1,0:T(8,128)S(1)}, u32[]{:S(2)}, u32[]{:S(2)}) collective-permute-start(f32[4,4,64,512]{3,2,1,0:T(8,128)} %get-tuple-element.83.refs_3_), channel_id=1, source_target_pairs={{0,1},{1,2},{2,3},{3,0},{4,5},{5,6},{6,7},{7,4},{8,9},{9,10},{10,1... | collective-permute-start | bytes 6291464 | tf_op jit(solution)/shard_map/ppermute | solution.py:765
  315.2 47.4 %collective-permute-start.24 = (f32[4,4,64,512]{3,2,1,0:T(8,128)}, f32[4,4,64,512]{3,2,1,0:T(8,128)S(1)}, u32[]{:S(2)}, u32[]{:S(2)}) collective-permute-start(f32[4,4,64,512]{3,2,1,0:T(8,128)} %get-tuple-element.82.refs_2_), channel_id=1, source_target_pairs={{0,3},{1,0},{2,1},{3,2},{4,7},{5,4},{6,5},{7,6},{8,11},{9,8},{10,9... | collective-permute-start | bytes 6291464 | tf_op jit(solution)/shard_map/ppermute | solution.py:765
  327.8 37.0 %copy-start.16 = (bf16[1024,256]{1,0:T(8,128)(2,1)S(1)}, bf16[1024,256]{1,0:T(8,128)(2,1)}, u32[]{:S(2)}) copy-start(bf16[1024,256]{1,0:T(8,128)(2,1)} %get-tuple-element.66) | copy-start | bytes 1572868
  327.8 97.5 %collective-permute-start.18 = (f32[4,4,72,512]{3,2,1,0:T(8,128)}, f32[4,4,72,512]{3,2,1,0:T(8,128)}, u32[]{:S(2)}, u32[]{:S(2)}) collective-permute-start(f32[4,4,72,512]{3,2,1,0:T(8,128)} %get-tuple-element.85.refs_5_), channel_id=1, source_target_pairs={{0,12},{4,0},{8,4},{12,8},{1,13},{5,1},{9,5},{13,9},{2,14},{6,2},{... | collective-permute-start | bytes 7077896 | tf_op jit(solution)/shard_map/ppermute | solution.py:765
  334.3 94.3 %collective-permute-start.22 = (f32[4,4,72,512]{3,2,1,0:T(8,128)}, f32[4,4,72,512]{3,2,1,0:T(8,128)}, u32[]{:S(2)}, u32[]{:S(2)}) collective-permute-start(f32[4,4,72,512]{3,2,1,0:T(8,128)} %get-tuple-element.85.refs_5_), channel_id=1, source_target_pairs={{0,4},{4,8},{8,12},{12,0},{1,5},{5,9},{9,13},{13,1},{2,6},{6,10},{... | collective-permute-start | bytes 7077896 | tf_op jit(solution)/shard_map/ppermute | solution.py:765
  336.3 92.3 %collective-permute-start.23 = (f32[4,4,72,512]{3,2,1,0:T(8,128)}, f32[4,4,72,512]{3,2,1,0:T(8,128)}, u32[]{:S(2)}, u32[]{:S(2)}) collective-permute-start(f32[4,4,72,512]{3,2,1,0:T(8,128)} %get-tuple-element.80.refs_0_), channel_id=1, source_target_pairs={{0,48},{16,0},{32,16},{48,32},{1,49},{17,1},{33,17},{49,33},{2,50}... | collective-permute-start | bytes 7077896 | tf_op jit(solution)/shard_map/ppermute | solution.py:765
  360.8 71.0 %collective-permute-start.8 = (f32[4,4,72,512]{3,2,1,0:T(8,128)}, f32[4,4,72,512]{3,2,1,0:T(8,128)}, u32[]{:S(2)}, u32[]{:S(2)}) collective-permute-start(f32[4,4,72,512]{3,2,1,0:T(8,128)} %get-tuple-element.80.refs_0_), channel_id=1, source_target_pairs={{0,16},{16,32},{32,48},{48,0},{1,17},{17,33},{33,49},{49,1},{2,18}... | collective-permute-start | bytes 7077896 | tf_op jit(solution)/shard_map/ppermute | solution.py:765
  362.6 62.6 %collective-permute-start.25 = (f32[4,4,64,512]{3,2,1,0:T(8,128)}, f32[4,4,64,512]{3,2,1,0:T(8,128)}, u32[]{:S(2)}, u32[]{:S(2)}) collective-permute-start(f32[4,4,64,512]{3,2,1,0:T(8,128)} %get-tuple-element.84.refs_4_), channel_id=1, source_target_pairs={{0,12},{4,0},{8,4},{12,8},{1,13},{5,1},{9,5},{13,9},{2,14},{6,2},{... | collective-permute-start | bytes 6291464 | tf_op jit(solution)/shard_map/ppermute | solution.py:765
  379.4 75.1 %copy-start.39 = (f32[512]{0:T(512)S(1)}, f32[512]{0:T(512)}, u32[]{:S(2)}) copy-start(f32[512]{0:T(512)} %param.22) | copy-start | bytes 6148
  425.3 25.8 %collective-permute-start.6 = (f32[1024,512]{1,0:T(8,128)}, f32[1024,512]{1,0:T(8,128)}, u32[]{:S(2)}, u32[]{:S(2)}) collective-permute-start(f32[1024,512]{1,0:T(8,128)} %add_add_fusion), channel_id=1, source_target_pairs={{0,64},{64,0},{1,65},{65,1},{2,66},{66,2},{3,67},{67,3},{4,68},{68... | collective-permute-start | bytes 6291464 | tf_op jit(solution)/shard_map/ppermute | solution.py:779
  425.3 49.2 %collective-permute-start.11 = (f32[4,4,64,512]{3,2,1,0:T(8,128)}, f32[4,4,64,512]{3,2,1,0:T(8,128)}, u32[]{:S(2)}, u32[]{:S(2)}) collective-permute-start(f32[4,4,64,512]{3,2,1,0:T(8,128)} %collective-permute-done.10.refs_7_), channel_id=1, source_target_pairs={{0,48},{16,0},{32,16},{48,32},{1,49},{17,1},{33,17},{49,33},{2,50}... | collective-permute-start | bytes 6291464 | tf_op jit(solution)/shard_map/ppermute | solution.py:765
  428.6 175.4 %collective-permute-start.13 = (f32[4,4,64,512]{3,2,1,0:T(8,128)}, f32[4,4,64,512]{3,2,1,0:T(8,128)}, u32[]{:S(2)}, u32[]{:S(2)}) collective-permute-start(f32[4,4,64,512]{3,2,1,0:T(8,128)} %collective-permute-done.12.refs_2_), channel_id=1, source_target_pairs={{0,1},{1,2},{2,3},{3,0},{4,5},{5,6},{6,7},{7,4},{8,9},{9,10},{10,1... | collective-permute-start | bytes 6291464 | tf_op jit(solution)/shard_map/ppermute | solution.py:765
  428.6 175.3 %collective-permute-start.15 = (f32[4,4,64,512]{3,2,1,0:T(8,128)}, f32[4,4,64,512]{3,2,1,0:T(8,128)}, u32[]{:S(2)}, u32[]{:S(2)}) collective-permute-start(f32[4,4,64,512]{3,2,1,0:T(8,128)} %collective-permute-done.14.refs_9_), channel_id=1, source_target_pairs={{0,3},{1,0},{2,1},{3,2},{4,7},{5,4},{6,5},{7,6},{8,11},{9,8},{10,9... | collective-permute-start | bytes 6291464 | tf_op jit(solution)/shard_map/ppermute | solution.py:765
  431.8 172.1 %collective-permute-start.17 = (f32[4,4,64,512]{3,2,1,0:T(8,128)}, f32[4,4,64,512]{3,2,1,0:T(8,128)}, u32[]{:S(2)}, u32[]{:S(2)}) collective-permute-start(f32[4,4,64,512]{3,2,1,0:T(8,128)} %collective-permute-done.16.refs_4_), channel_id=1, source_target_pairs={{0,4},{4,8},{8,12},{12,0},{1,5},{5,9},{9,13},{13,1},{2,6},{6,10},{... | collective-permute-start | bytes 6291464 | tf_op jit(solution)/shard_map/ppermute | solution.py:765
  451.1 152.8 %collective-permute-start.19 = (f32[4,4,72,512]{3,2,1,0:T(8,128)}, f32[4,4,72,512]{3,2,1,0:T(8,128)}, u32[]{:S(2)}, u32[]{:S(2)}) collective-permute-start(f32[4,4,72,512]{3,2,1,0:T(8,128)} %collective-permute-done.18.refs_11_), channel_id=1, source_target_pairs={{0,12},{4,0},{8,4},{12,8},{1,13},{5,1},{9,5},{13,9},{2,14},{6,2},{... | collective-permute-start | bytes 7077896 | tf_op jit(solution)/shard_map/ppermute | solution.py:765
  474.5 129.5 %collective-permute-start.9 = (f32[4,4,72,512]{3,2,1,0:T(8,128)}, f32[4,4,72,512]{3,2,1,0:T(8,128)}, u32[]{:S(2)}, u32[]{:S(2)}) collective-permute-start(f32[4,4,72,512]{3,2,1,0:T(8,128)} %collective-permute-done.8.refs_0_), channel_id=1, source_target_pairs={{0,16},{16,32},{32,48},{48,0},{1,17},{17,33},{33,49},{49,1},{2,18}... | collective-permute-start | bytes 7077896 | tf_op jit(solution)/shard_map/ppermute | solution.py:765
  (45 other events, 232.5 us)
